TPU v7x, 32 devices: a whole 2x2x4 slice. The times are simulated.
32 devices in a mesh: seq: 16 (over z, x, core), zero: 2 (over y).
Axes of the slice: x: 2, y: 2, z: 4, core: 2. Of those that a mesh axis runs over, the one named last changes fastest.
Arguments:
- tokens: bfloat16 [2, 2048, 2048], P('zero', 'seq'), may hold values from -6 to 6
- w_in: bfloat16 [2048, 2336], P('zero'), may hold values from -0.0625 to 0.0625
- a_log: float32 [32], replicated, may hold values from -8 to 0
- dt_bias: float32 [32], replicated, may hold values from -4.5 to -3.5
- d_skip: float32 [32], replicated, may hold values from 0.5 to 1.5
- grad_y: bfloat16 [2, 2048, 2048], P('zero', 'seq'), may hold values from -6 to 6
Outputs:
- y_out: bfloat16 [2, 2048, 2048], P('zero', 'seq')
- grad_tokens: bfloat16 [2, 2048, 2048], P('zero', 'seq')
- grad_w: float32 [2048, 2336], P(('seq', 'zero'))
All inputs are finite; a program needn't handle non-finite values.
Results may differ from a plain program's by a relative error of at most 0.013.
Values may be sent and summed in bfloat16 or wider, within the bound.
A program may use at most 128 MiB of HBM per device.

v0:
```python
import functools

import jax
import jax.numpy as jnp
from jax import lax
from jax.experimental import pallas as pl
from jax.experimental.pallas import tpu as pltpu
from jax.sharding import PartitionSpec as P

BF = jnp.bfloat16
F32 = jnp.float32
MESH = pl.DeviceIdType.MESH


def shift(value, axis, step):
    count = lax.axis_size(axis)
    return lax.ppermute(value, axis, [(i, (i + step) % count) for i in range(count)])


def dot(a, b, dims):
    return lax.dot_general(a, b, (dims, ((), ())), preferred_element_type=F32)


def bdot(a, b, spec):
    return jnp.einsum(spec, a, b, preferred_element_type=F32)


def greet(peers):
    barrier = pltpu.get_barrier_semaphore()
    for peer in peers:
        pl.semaphore_signal(barrier, inc=1, device_id={"seq": peer}, device_id_type=MESH)
    pl.semaphore_wait(barrier, len(peers))


def remote(src, dst, send, recv, peer):
    return pltpu.make_async_remote_copy(
        src_ref=src,
        dst_ref=dst,
        send_sem=send,
        recv_sem=recv,
        device_id={"seq": peer},
        device_id_type=MESH,
    )


def scan_kernel(
    pair, totals, start, end, both, marks, joined, sums, got, lengths, made, back, final, wide,
    send, recv, local
):
    chips, _, share = pair.shape[:3]
    me = lax.axis_index("seq")
    core, chip = lax.rem(me, 2), lax.div(me, 2)
    sibling = me + 1 - 2 * core
    places = [lax.rem(chip + d, chips) for d in range(1, chips)]
    peers = [place * 2 + core for place in places]
    greet([sibling] + peers)

    def move(copies):
        for copy in copies:
            copy.start()
        for copy in copies:
            copy.wait()

    move(
        [
            remote(pair.at[:, 1 - core], both.at[core], send.at[0, 0], recv.at[0, 0], sibling),
            remote(totals.at[:, 1 - core], marks.at[core], send.at[1, 0], recv.at[1, 0], sibling),
            pltpu.make_async_copy(pair.at[:, core], both.at[core], local.at[0]),
            pltpu.make_async_copy(totals.at[:, core], marks.at[core], local.at[1]),
        ]
    )

    def gain(ref, *at):
        return jnp.exp(ref[at])

    for k in range(chips):
        sums[k] = marks[0, k] + marks[1, k]
        for j in range(share):
            row = pl.ds(j, 1)
            joined[k, j, 0] = (
                gain(marks, 1, k, row) * both[0, k, j, 0].astype(F32)
                + both[1, k, j, 0].astype(F32)
            ).astype(BF)
            joined[k, j, 1] = (
                gain(marks, 0, k, row) * both[1, k, j, 1].astype(F32)
                + both[0, k, j, 1].astype(F32)
            ).astype(BF)
    copies = []
    for d, (place, peer) in enumerate(zip(places, peers)):
        copies.append(remote(joined.at[place], got.at[chip], send.at[2, d], recv.at[2, d], peer))
        copies.append(remote(sums.at[place], lengths.at[chip], send.at[3, d], recv.at[3, d], peer))
    copies.append(pltpu.make_async_copy(joined.at[chip], got.at[chip], local.at[2]))
    copies.append(pltpu.make_async_copy(sums.at[chip], lengths.at[chip], local.at[3]))
    move(copies)

    for j in range(share):
        row = pl.ds(j, 1)
        run = jnp.zeros(pair.shape[4:], F32)
        for k in range(chips):
            made[k, j, 0] = run.astype(BF)
            if k < chips - 1:
                run = gain(lengths, k, row) * run + got[k, j, 0].astype(F32)
        run = jnp.zeros(pair.shape[4:], F32)
        for k in reversed(range(chips)):
            made[k, j, 1] = run.astype(BF)
            if k > 0:
                run = gain(lengths, k, row) * run + got[k, j, 1].astype(F32)
    copies = [
        remote(made.at[place], back.at[chip], send.at[4, d], recv.at[4, d], peer)
        for d, (place, peer) in enumerate(zip(places, peers))
    ]
    move(copies + [pltpu.make_async_copy(made.at[chip], back.at[chip], local.at[4])])

    for k in range(chips):
        for j in range(share):
            row = pl.ds(j, 1)
            first, last = back[k, j, 0], back[k, j, 1]
            final[0, k, j, 0] = first
            final[1, k, j, 1] = last
            final[1, k, j, 0] = (
                gain(marks, 0, k, row) * first.astype(F32) + both[0, k, j, 0].astype(F32)
            ).astype(BF)
            final[0, k, j, 1] = (
                gain(marks, 1, k, row) * last.astype(F32) + both[1, k, j, 1].astype(F32)
            ).astype(BF)
    move(
        [
            remote(final.at[1 - core], wide.at[core], send.at[5, 0], recv.at[5, 0], sibling),
            pltpu.make_async_copy(final.at[core], wide.at[core], local.at[5]),
        ]
    )
    for parity in range(2):
        start[:, parity] = wide[parity, :, :, 0]
        end[:, parity] = wide[parity, :, :, 1]


def scan_states(pair, totals):
    chips, _, share, _, rows, lanes = pair.shape
    state = jax.ShapeDtypeStruct((chips, 2, share, rows, lanes), BF)
    half = (chips,) + pair.shape[2:]
    short = (chips,) + totals.shape[2:]
    return pl.pallas_call(
        scan_kernel,
        out_shape=(state, state),
        in_specs=[pl.BlockSpec(memory_space=pltpu.VMEM)] * 2,
        out_specs=[pl.BlockSpec(memory_space=pltpu.VMEM)] * 2,
        scratch_shapes=[
            pltpu.VMEM((2,) + half, BF),
            pltpu.VMEM((2,) + short, F32),
            pltpu.VMEM(half, BF),
            pltpu.VMEM(short, F32),
            pltpu.VMEM(half, BF),
            pltpu.VMEM(short, F32),
            pltpu.VMEM(half, BF),
            pltpu.VMEM(half, BF),
            pltpu.VMEM((2,) + half, BF),
            pltpu.VMEM((2,) + half, BF),
            pltpu.SemaphoreType.DMA((6, chips)),
            pltpu.SemaphoreType.DMA((6, chips)),
            pltpu.SemaphoreType.DMA((6,)),
        ],
        compiler_params=pltpu.CompilerParams(collective_id=0, has_side_effects=True),
    )(pair, totals)


def sum_kernel(seq, spans, tile, left, right, out, *scratch):
    levels = (seq // 2).bit_length() - 1
    me = lax.axis_index("seq")
    core, place = lax.rem(me, 2), lax.div(me, 2)
    bits = [lax.rem(lax.div(place, 1 << b), 2) for b in range(levels)]
    sibling = me + 1 - 2 * core
    partners = [me + (1 - 2 * bits[b]) * (2 << b) for b in range(levels)]
    greet([sibling] + partners)
    pieces, piece, tokens = left.shape[1:]
    parts = len(spans)
    up = list(range(levels))
    orders = [up, up[1:] + up[:1]] * (parts // 2)
    acc, away, come = (scratch[i * parts : (i + 1) * parts] for i in range(3))
    rest = scratch[3 * parts : -2]
    outs = [rest[h * levels : (h + 1) * levels] for h in range(parts)]
    ins = [rest[(parts + h) * levels : (parts + h + 1) * levels] for h in range(parts)]
    send, recv = scratch[-2:]

    def multiply(side, h, target):
        low, high = spans[h]
        rows = left[side].reshape(pieces * piece, tokens)
        full = (high - low) // tile

        def column(first, own, wide):
            made = jnp.dot(rows, right[:, pl.ds(first, wide)], preferred_element_type=F32)
            target[:, :, pl.ds(own, wide)] = made.reshape(pieces, piece, wide).astype(target.dtype)

        @pl.loop(0, full)
        def _(i):
            own = pl.multiple_of(i * tile, 128)
            column(pl.multiple_of(low + i * tile, 128), own, tile)

        if (high - low) % tile:
            column(low + full * tile, full * tile, (high - low) % tile)

    first = []
    for h in range(parts):
        multiply(1 - core, h, away[h])
        copy = remote(away[h], come[h], send.at[h, levels], recv.at[h, levels], sibling)
        copy.start()
        first.append(copy)

    def subsets(rest):
        found = [0]
        for b in rest:
            found = found + [value + (1 << b) for value in found]
        return found

    def begin(h, s):
        order = orders[h]
        b = order[s]
        base = sum((bits[f] * (1 << f) for f in order[:s]), 0)
        for j, extra in enumerate(subsets(order[s + 1 :])):
            outs[h][s][j] = acc[h][base + (1 - bits[b]) * (1 << b) + extra].astype(BF)
        copy = remote(outs[h][s], ins[h][s], send.at[h, s], recv.at[h, s], partners[b])
        copy.start()
        return copy

    def finish(h, s, copy):
        copy.wait()
        order = orders[h]
        base = sum((bits[f] * (1 << f) for f in order[: s + 1]), 0)
        for j, extra in enumerate(subsets(order[s + 1 :])):
            acc[h][base + extra] += ins[h][s][j].astype(F32)

    flying = []
    for h in range(parts):
        multiply(core, h, acc[h])
        first[h].wait()

        @pl.loop(0, pieces)
        def _(i):
            acc[h][i] += come[h][i].astype(F32)

        flying.append(begin(h, 0))
    for s in range(levels):
        for h in range(parts):
            finish(h, s, flying[h])
            if s + 1 < levels:
                flying[h] = begin(h, s + 1)
    for h in range(parts):
        out[:, spans[h][0] : spans[h][1]] = acc[h][place]


def sum_shards(left, right):
    pieces, piece = left.shape[1:3]
    cols = right.shape[1]
    seq = 2 * pieces
    tile, parts = 384, 6
    levels = pieces.bit_length() - 1
    edges = [(2 * i * cols // parts + 128) // 256 * 128 for i in range(parts)] + [cols]
    spans = list(zip(edges[:-1], edges[1:]))
    widths = [high - low for low, high in spans]
    scratch = [pltpu.VMEM((pieces, piece, w), F32) for w in widths]
    scratch += [pltpu.VMEM((pieces, piece, w), BF) for w in widths] * 2
    for _ in range(2):
        for w in widths:
            scratch += [pltpu.VMEM((pieces >> (s + 1), piece, w), BF) for s in range(levels)]
    scratch += [pltpu.SemaphoreType.DMA((parts, levels + 1))] * 2
    return pl.pallas_call(
        functools.partial(sum_kernel, seq, spans, tile),
        out_shape=jax.ShapeDtypeStruct((piece, cols), F32),
        in_specs=[pl.BlockSpec(memory_space=pltpu.VMEM)] * 2,
        out_specs=pl.BlockSpec(memory_space=pltpu.VMEM),
        scratch_shapes=scratch,
        compiler_params=pltpu.CompilerParams(collective_id=1, has_side_effects=True),
    )(left, right)


def ssd_block(proj, gy, a_log, dt_bias, d_skip):
    count, inner = gy.shape
    heads = a_log.shape[0]
    width = inner // heads
    size = (proj.shape[1] - inner - heads) // 2
    xs = proj[:, :inner].astype(BF)
    bm = proj[:, inner : inner + size].astype(BF)
    cm = proj[:, inner + size : inner + 2 * size].astype(BF)
    raw = proj[:, inner + 2 * size :] + dt_bias
    dt = jax.nn.softplus(raw)
    rate = -jnp.exp(a_log)
    lower = jnp.arange(count)[:, None] >= jnp.arange(count)[None, :]
    cum = jnp.dot(lower.astype(F32), rate * dt, precision=lax.Precision.HIGHEST)
    total = cum[-1]
    growth = jnp.exp(cum)
    fade = jnp.exp(total - cum)
    x3 = xs.reshape(count, heads, width).astype(F32)
    g3 = gy.reshape(count, heads, width).astype(F32)
    xd = (x3 * dt[:, :, None]).astype(BF)
    grown = (g3 * growth[:, :, None]).astype(BF).reshape(count, inner)
    faded = (xd.astype(F32) * fade[:, :, None]).astype(BF).reshape(count, inner)
    local_f = dot(faded, bm, ((0,), (0,)))
    local_g = dot(grown, cm, ((0,), (0,)))
    shape = (heads, width, size)
    pair = jnp.stack([local_f.reshape(shape), local_g.reshape(shape)], axis=1).astype(BF)

    seq = lax.axis_size("seq")
    share = heads // seq
    marks = jnp.pad(total.reshape(seq, share), ((0, 0), (0, -share % 8)))
    marks = jnp.broadcast_to(marks[:, :, None], marks.shape + (size,))
    marks = marks.reshape(seq // 2, 2, -1, size)
    start, end = scan_states(pair.reshape(seq // 2, 2, share, 2, width, size), marks)
    start, end = start.reshape(inner, size), end.reshape(inner, size)

    spans = cum.T[:, :, None] - cum.T[:, None, :]
    decay = jnp.where(lower[None], jnp.exp(jnp.where(lower[None], spans, 0.0)), 0.0)
    scores = dot(cm, bm, ((1,), (1,)))
    mixing = (scores[None] * decay).astype(BF)
    gb3 = gy.reshape(count, heads, width)
    y_in = bdot(mixing, xd, "hts,shp->thp")
    back_in = bdot(mixing, gb3, "hts,thp->shp")
    cross = bdot(gb3, xd, "thp,shp->hts")
    mixed = jnp.sum(cross * decay, axis=0).astype(BF)

    y3 = y_in + dot(cm, start, ((1,), (1,))).reshape(x3.shape) * growth[:, :, None]
    h3 = back_in + dot(bm, end, ((1,), (1,))).reshape(x3.shape) * fade[:, :, None]
    out = y3 + d_skip[:, None] * x3
    grad_x = h3 * dt[:, :, None] + d_skip[:, None] * g3
    grad_c = dot(mixed, bm, ((1,), (0,))) + dot(grown, start, ((1,), (0,)))
    grad_b = dot(mixed, cm, ((0,), (0,))) + dot(faded, end, ((1,), (0,)))
    row = jnp.sum(g3 * y3, axis=2)
    column = jnp.sum(xd.astype(F32) * h3, axis=2)
    grad_dt = jnp.sum(x3 * h3, axis=2)
    joint = jnp.sum((start.astype(F32) * end.astype(F32)).reshape(heads, -1), axis=1)
    tail = jnp.sum(
        xd.astype(F32) * dot(bm, end, ((1,), (1,))).reshape(x3.shape) * fade[:, :, None], axis=(0, 2)
    )
    last = tail + jnp.exp(total) * joint
    grad_log = jnp.dot(
        lower.astype(F32).T, row - column, precision=lax.Precision.HIGHEST
    ) + last
    grad_raw = (grad_dt + grad_log * rate) * jax.nn.sigmoid(raw)
    gproj = jnp.concatenate(
        [grad_x.reshape(count, inner), grad_b, grad_c, grad_raw], axis=1
    ).astype(BF)
    return out.reshape(count, inner).astype(BF), gproj


def per_device(tokens, w_in, a_log, dt_bias, d_skip, grad_y):
    count, width = tokens.shape[1:]
    inner = grad_y.shape[2]
    heads = a_log.shape[0]
    columns = w_in.shape[1]
    exact = columns - heads
    zero = lax.axis_size("zero")
    seq = lax.axis_size("seq")
    here = lax.axis_index("zero")
    owned = width // zero
    rows = tokens.reshape(count, width)

    def columns_of(z):
        return lax.dynamic_slice_in_dim(rows, z * owned, owned, axis=1)

    guests = [shift(columns_of((here + s) % zero), "zero", s) for s in range(1, zero)]
    proj = jnp.dot(columns_of(here), w_in, preferred_element_type=F32)
    for s, guest in zip(range(1, zero), guests):
        part = jnp.dot(guest, w_in, preferred_element_type=F32)
        wide = shift(part[:, :exact].astype(BF), "zero", zero - s)
        narrow = shift(part[:, exact:], "zero", zero - s)
        proj = proj + jnp.concatenate([wide.astype(F32), narrow], axis=1)

    piece = width // (seq * zero)
    cut = rows.reshape(count, seq, zero, piece)

    def pieces_of(z):
        return lax.dynamic_index_in_dim(cut, z, 2, keepdims=False).reshape(count, seq * piece)

    theirs = [shift(pieces_of((here + s) % zero), "zero", s) for s in range(1, zero)]

    y_out, gproj = ssd_block(proj, grad_y.reshape(count, inner), a_log, dt_bias, d_skip)

    others = [shift(gproj, "zero", s) for s in range(1, zero)]
    mine = dot(gproj, w_in, ((1,), (1,))).astype(BF)
    grads = [mine]
    for s, other in zip(range(1, zero), others):
        grads.append(shift(dot(other, w_in, ((1,), (1,))).astype(BF), "zero", zero - s))
    blocks = []
    for z in range(zero):
        block = grads[0]
        for s in range(1, zero):
            block = jnp.where((here + s) % zero == z, grads[s], block)
        blocks.append(block)
    grad_tokens = jnp.concatenate(blocks, axis=1).reshape(1, count, width)

    left = jnp.concatenate([pieces_of(here)] + theirs, axis=0)
    right = jnp.concatenate([gproj] + others, axis=0)
    left = left.reshape(left.shape[0], seq // 2, 2, piece).transpose(2, 1, 3, 0)
    grad_w = sum_shards(left, right)
    return (y_out.reshape(1, count, inner), grad_tokens, grad_w)


def solution(mesh):
    placed = (P("zero", "seq", None), P("zero", None), P(), P(), P(), P("zero", "seq", None))
    return jax.shard_map(
        per_device,
        mesh=mesh,
        in_specs=placed,
        out_specs=(P("zero", "seq", None), P("zero", "seq", None), P(("seq", "zero"), None)),
        check_vma=False,
    )
```

profile of v0, /device:TPU:0, one launch (start us, length us, event | category | flops | bytes accessed | tf_op | source)
XLA Modules:
  0.0 176.2 jit_solution(4395038813758033001)
XLA Ops:
  0.6 1.0 dynamic-slice_bitcast_fusion
  1.6 3.1 %collective-permute-start = (bf16[128,1024]{1,0:T(8,128)(2,1)S(1)}, bf16[128,1024]{1,0:T(8,128)(2,1)S(1)}, u32[]{:S(2)}, u32[]{:S(2)}) collective-permute-start(bf16[128,1024]{1,0:T(8,128)(2,1)S(1)} %dynamic-slice_bitcast_fusion), channel_id=1, source_target_pairs={{0,1},{1,0},{2,3},{3,2},{4,5},{5,4},{6,7},{7,6},{8,9},{9,8},{10,11... | collective-permute-start | bytes 786440 | tf_op jit(solution)/shard_map/ppermute | solution.py:17
  4.7 6.3 %collective-permute-done = bf16[128,1024]{1,0:T(8,128)(2,1)S(1)} collective-permute-done((bf16[128,1024]{1,0:T(8,128)(2,1)S(1)}, bf16[128,1024]{1,0:T(8,128)(2,1)S(1)}, u32[]{:S(2)}, u32[]{:S(2)}) %collective-permute-start) | collective-permute-done | bytes 262176 | tf_op jit(solution)/shard_map/ppermute | solution.py:17
  11.0 3.8 %fusion.49 = f32[128,2336]{0,1:T(8,128)S(1)} fusion(bf16[128,1024]{1,0:T(8,128)(2,1)S(1)} %collective-permute-done, bf16[1024,2336]{0,1:T(8,128)(2,1)} %param.7), kind=kOutput, calls=%fused_computation.93 | convolution fusion | flops 612368384 | bytes 6242304 | tf_op jit(solution)/shard_map/dot_general | solution.py:361
  14.8 1.1 copy.127
  15.9 1.7 collective-permute-start.1
  17.7 0.3 copy.110
  17.9 0.7 constant_dynamic-slice_fusion.1
  18.7 0.3 collective-permute-start.5
  19.0 0.1 copy.128
  19.1 1.8 %collective-permute-start.2 = (f32[128,32]{1,0:T(8,128)S(1)}, f32[128,32]{1,0:T(8,128)S(1)}, u32[]{:S(2)}, u32[]{:S(2)}) collective-permute-start(f32[128,32]{1,0:T(8,128)S(1)} %copy.128), channel_id=1, source_target_pairs={{0,1},{1,0},{2,3},{3,2},{4,5},{5,4},{6,7},{7,6},{8,9},{9,8},{10,11... | collective-permute-start | bytes 49160 | tf_op jit(solution)/shard_map/ppermute | solution.py:17
  20.9 1.3 copy.99
  22.2 10.1 %collective-permute-done.1 = bf16[128,2304]{1,0:T(8,128)(2,1)S(1)} collective-permute-done((bf16[128,2304]{1,0:T(8,128)(2,1)}, bf16[128,2304]{1,0:T(8,128)(2,1)S(1)}, u32[]{:S(2)}, u32[]{:S(2)}) %collective-permute-start.1) | collective-permute-done | bytes 589856 | tf_op jit(solution)/shard_map/ppermute | solution.py:17
  32.4 5.2 %collective-permute-done.2 = f32[128,32]{1,0:T(8,128)S(1)} collective-permute-done((f32[128,32]{1,0:T(8,128)S(1)}, f32[128,32]{1,0:T(8,128)S(1)}, u32[]{:S(2)}, u32[]{:S(2)}) %collective-permute-start.2) | collective-permute-done | bytes 16416 | tf_op jit(solution)/shard_map/ppermute | solution.py:17
  37.6 4.1 %fusion.48 = (bf16[128,2336]{1,0:T(8,128)(2,1)S(1)}, f32[128,2336]{1,0:T(8,128)S(1)}) fusion(f32[128,32]{1,0:T(8,128)S(1)} %collective-permute-done.2, f32[128,2304]{1,0:T(8,128)S(1)} %convert_element_type.107, bf16[1024,2336]{0,1:T(8,128)(2,1)} %param.7, bf16[1,128,2048]{2,1,0:T(8,128)(2,1)S(1)} %copy-done.3, s32[]{:T(128)S(6)} %select_n.51), kind=kOutput, calls=%fused_computation.92 | convolution fusion | flops 613265408 | bytes 8085508 | tf_op jit(solution)/shard_map/dot_general | solution.py:359
  41.7 1.2 slice_convert_fusion.1
  42.9 0.1 fusion.35
  43.0 0.1 copy-done.4
  43.2 0.2 fusion.24
  43.5 0.2 slice_reduce_fusion
  43.7 0.1 subtract_exponential_fusion
  43.8 1.1 mul.147
  44.9 1.6 copy.97
  46.4 1.1 mul.139
  47.5 2.5 %copy.95 = f32[128,2048]{1,0:T(8,128)} copy(f32[128,2048]{0,1:T(8,128)} %bitcast.111) | data formatting | bytes 2097152 | tf_op jit(solution)/shard_map/mul | solution.py:293
  50.0 1.4 multiply_convert_fusion.1
  51.4 0.3 copy.98
  51.7 0.3 fusion.3
  52.0 0.1 fusion.18
  52.1 0.3 fusion.4
  52.4 0.1 reshape_squeeze.3
  52.5 1.1 pad_maximum_fusion.1.pair
  53.6 0.7 broadcast_in_dim.25.totals
  54.3 33.2 %shard_map.85 = (bf16[8,2,2,64,128]{4,3,2,1,0:T(8,128)(2,1)}, bf16[8,2,2,64,128]{4,3,2,1,0:T(8,128)(2,1)}) custom-call(bf16[8,2,2,2,64,128]{5,4,3,2,1,0:T(8,128)(2,1)} %pad_maximum_fusion.1.pair, f32[8,2,8,128]{3,2,1,0:T(8,128)} %broadcast_in_dim.25.totals), custom_call_target="tpu_custom_call" | custom-call | tf_op jit(solution)/shard_map/pallas_call | solution.py:142
  87.5 2.3 %fusion.28 = f32[128,32,64]{0,2,1:T(8,128)} fusion(bf16[32,64,128]{2,1,0:T(8,128)(2,1)} %bitcast.105, bf16[128,2336]{1,0:T(8,128)(2,1)S(1)} %get-tuple-element.35), kind=kOutput, calls=%fused_computation.66 | convolution fusion | flops 67108864 | bytes 1605632 | tf_op jit(solution)/shard_map/dot_general | solution.py:21
  89.8 1.5 copy.90
  91.4 3.9 %fusion.11 = (f32[128,32]{0,1:T(8,128)}, f32[128,32]{0,1:T(8,128)}, f32[32]{0:T(128)}, bf16[128,32,64]{0,2,1:T(8,128)(2,1)S(1)}, bf16[128,32,64]{0,2,1:T(8,128)(2,1)}) fusion(f32[128,2048]{0,1:T(8,128)S(1)} %copy.90, f32[128,32]{0,1:T(8,128)S(1)} %get-tuple-element.33, f32[128,32,64]{0,2,1:T(8,128)} %fusion.28, f32[128,32,64]{0,2,1:T(8,128)S(1)} %bitcast.108, ...), kind=kOutput, calls=%fused_computation.32 | convolution fusion | flops 74178528 | bytes 4882688 | tf_op jit(solution)/shard_map/hts,thp->shp/dot_general | solution.py:25
  95.3 1.1 fusion
  96.4 0.8 convolution_bitcast_fusion.1
  97.2 0.2 copy-done.1
  97.4 0.3 fusion.50
  97.7 0.8 multiply_reduce_fusion
  98.6 0.1 fusion.8
  98.7 1.1 fusion.17
  99.9 0.3 fusion.51
  100.2 0.2 fusion.9
  100.4 0.8 reduce_sum.65
  101.2 0.8 copy.107
  102.0 1.2 copy.108
  103.3 1.0 fusion.10
  104.4 0.3 copy.109
  104.7 1.6 collective-permute-start.3
  106.3 1.8 %copy_bitcast_fusion.left = bf16[2,8,64,256]{3,2,1,0:T(8,128)(2,1)} fusion(bf16[128,8,2,64]{0,3,2,1:T(8,128)(2,1)} %bitcast.39, bf16[128,8,2,64]{0,3,2,1:T(8,128)(2,1)S(1)} %bitcast.117), kind=kLoop, calls=%fused_computation.52 | loop fusion | flops 1048576 | bytes 1048576 | tf_op jit(solution)/shard_map/transpose | solution.py:391
  108.1 1.0 copy.114
  109.1 3.2 %convolution_convert_fusion.2 = bf16[128,1024]{1,0:T(8,128)(2,1)S(1)} fusion(bf16[1024,2336]{0,1:T(8,128)(2,1)} %param.7, bf16[128,32]{1,0:T(8,128)(2,1)S(1)} %fusion.10, bf16[128,128]{1,0:T(8,128)(2,1)S(1)} %fusion.9, bf16[128,128]{1,0:T(8,128)(2,1)S(1)} %fusion.8, bf16[128,2048]{1,0:T(8,128)(2,1)S(1)} %copy.108), kind=kOutput, calls=%fused_computation.20 | convolution fusion | flops 614891520 | bytes 5644288 | tf_op jit(solution)/shard_map/dot_general | solution.py:21
  112.3 8.2 %collective-permute-done.3 = bf16[128,2336]{0,1:T(8,128)(2,1)S(1)} collective-permute-done((bf16[128,2336]{0,1:T(8,128)(2,1)S(1)}, bf16[128,2336]{0,1:T(8,128)(2,1)S(1)}, u32[]{:S(2)}, u32[]{:S(2)}) %collective-permute-start.3) | collective-permute-done | bytes 598048 | tf_op jit(solution)/shard_map/ppermute | solution.py:17
  120.5 3.2 %convolution_convert_fusion.3 = bf16[128,1024]{1,0:T(8,128)(2,1)S(1)} fusion(bf16[128,2336]{0,1:T(8,128)(2,1)S(1)} %collective-permute-done.3, bf16[1024,2336]{0,1:T(8,128)(2,1)} %param.7), kind=kOutput, calls=%fused_computation.21 | convolution fusion | flops 612499456 | bytes 5644288 | tf_op jit(solution)/shard_map/dot_general | solution.py:21
  123.8 1.6 collective-permute-start.4
  125.4 0.3 copy.113
  125.7 1.2 pad_maximum_fusion.right
  126.8 47.3 %shard_map.86 = f32[64,2336]{1,0:T(8,128)} custom-call(bf16[2,8,64,256]{3,2,1,0:T(8,128)(2,1)} %copy_bitcast_fusion.left, bf16[256,2336]{1,0:T(8,128)(2,1)} %pad_maximum_fusion.right), custom_call_target="tpu_custom_call" | custom-call | tf_op jit(solution)/shard_map/pallas_call | solution.py:265
  174.2 0.8 maximum_bitcast_fusion
  175.1 0.3 copy-done.2
  175.4 0.8 copy.133
  (45 shorter events, 0.5 us)
Async XLA Ops:
  1.6 9.4 %collective-permute-start = (bf16[128,1024]{1,0:T(8,128)(2,1)S(1)}, bf16[128,1024]{1,0:T(8,128)(2,1)S(1)}, u32[]{:S(2)}, u32[]{:S(2)}) collective-permute-start(bf16[128,1024]{1,0:T(8,128)(2,1)S(1)} %dynamic-slice_bitcast_fusion), channel_id=1, source_target_pairs={{0,1},{1,0},{2,3},{3,2},{4,5},{5,4},{6,7},{7,6},{8,9},{9,8},{10,11... | collective-permute-start | bytes 786440 | tf_op jit(solution)/shard_map/ppermute | solution.py:17
  14.8 2.9 %copy-start.3 = (bf16[1,128,2048]{2,1,0:T(8,128)(2,1)S(1)}, bf16[1,128,2048]{2,1,0:T(8,128)(2,1)}, u32[]{:S(2)}) copy-start(bf16[1,128,2048]{2,1,0:T(8,128)(2,1)} %param.6) | copy-start | bytes 1572868
  14.8 4.2 %copy-start.15 = (f32[32]{0:T(128)S(1)}, f32[32]{0:T(128)}, u32[]{:S(2)}) copy-start(f32[32]{0:T(128)} %param.8) | copy-start | bytes 388
  15.9 16.4 %collective-permute-start.1 = (bf16[128,2304]{1,0:T(8,128)(2,1)}, bf16[128,2304]{1,0:T(8,128)(2,1)S(1)}, u32[]{:S(2)}, u32[]{:S(2)}) collective-permute-start(bf16[128,2304]{1,0:T(8,128)(2,1)} %copy.127), channel_id=1, source_target_pairs={{0,1},{1,0},{2,3},{3,2},{4,5},{5,4},{6,7},{7,6},{8,9},{9,8},{10,11... | collective-permute-start | bytes 1769480 | tf_op jit(solution)/shard_map/ppermute | solution.py:17
  18.7 87.6 %collective-permute-start.5 = (bf16[128,1024]{0,1:T(8,128)(2,1)}, bf16[128,1024]{0,1:T(8,128)(2,1)}, u32[]{:S(2)}, u32[]{:S(2)}) collective-permute-start(bf16[128,1024]{0,1:T(8,128)(2,1)} %bitcast.38), channel_id=1, source_target_pairs={{0,1},{1,0},{2,3},{3,2},{4,5},{5,4},{6,7},{7,6},{8,9},{9,8},{10,11... | collective-permute-start | bytes 786440 | tf_op jit(solution)/shard_map/ppermute | solution.py:17
  19.0 24.2 %copy-start.12 = (f32[32]{0:T(128)}, f32[32]{0:T(128)S(1)}, u32[]{:S(2)}) copy-start(f32[32]{0:T(128)S(1)} %exponential_negate_fusion) | copy-start | bytes 388
  19.1 18.5 %collective-permute-start.2 = (f32[128,32]{1,0:T(8,128)S(1)}, f32[128,32]{1,0:T(8,128)S(1)}, u32[]{:S(2)}, u32[]{:S(2)}) collective-permute-start(f32[128,32]{1,0:T(8,128)S(1)} %copy.128), channel_id=1, source_target_pairs={{0,1},{1,0},{2,3},{3,2},{4,5},{5,4},{6,7},{7,6},{8,9},{9,8},{10,11... | collective-permute-start | bytes 49160 | tf_op jit(solution)/shard_map/ppermute | solution.py:17
  32.4 10.7 %copy-start.10 = (f32[32]{0:T(128)S(1)}, f32[32]{0:T(128)}, u32[]{:S(2)}) copy-start(f32[32]{0:T(128)} %param.9) | copy-start | bytes 388
  41.7 1.4 copy-start.4
  43.7 3.8 %copy-start.6 = (f32[1,32]{1,0:T(1,128)}, f32[1,32]{1,0:T(1,128)S(1)}, u32[]{:S(2)}) copy-start(f32[1,32]{1,0:T(1,128)S(1)} %copy.129) | copy-start | bytes 388
  87.5 3.9 %copy-start.8 = (f32[32]{0:T(128)S(1)}, f32[32]{0:T(128)}, u32[]{:S(2)}) copy-start(f32[32]{0:T(128)} %param.10) | copy-start | bytes 388
  96.4 1.0 copy-start.1
  96.4 1.3 copy-start
  97.2 1.5 copy-start.9
  99.8 3.4 %copy-start.7 = (f32[1,32]{1,0:T(1,128)S(1)}, f32[1,32]{1,0:T(1,128)}, u32[]{:S(2)}) copy-start(f32[1,32]{1,0:T(1,128)} %copy-done.6) | copy-start | bytes 388
  99.8 3.4 %copy-start.14 = (f32[32]{0:T(128)S(1)}, f32[32]{0:T(128)}, u32[]{:S(2)}) copy-start(f32[32]{0:T(128)} %get-tuple-element.21) | copy-start | bytes 388
  99.8 3.5 %copy-start.5 = (f32[128,32]{0,1:T(8,128)S(1)}, f32[128,32]{0,1:T(8,128)}, u32[]{:S(2)}) copy-start(f32[128,32]{0,1:T(8,128)} %get-tuple-element.24) | copy-start | bytes 49156
  99.8 3.5 %copy-start.11 = (f32[32]{0:T(128)S(1)}, f32[32]{0:T(128)}, u32[]{:S(2)}) copy-start(f32[32]{0:T(128)} %param.9) | copy-start | bytes 388
  99.8 3.5 %copy-start.13 = (f32[32]{0:T(128)S(1)}, f32[32]{0:T(128)}, u32[]{:S(2)}) copy-start(f32[32]{0:T(128)} %copy-done.12) | copy-start | bytes 388
  99.8 3.5 %copy-start.16 = (f32[128,32]{0,1:T(8,128)S(1)}, f32[128,32]{0,1:T(8,128)}, u32[]{:S(2)}) copy-start(f32[128,32]{0,1:T(8,128)} %get-tuple-element.19) | copy-start | bytes 49156
  104.7 15.8 %collective-permute-start.3 = (bf16[128,2336]{0,1:T(8,128)(2,1)S(1)}, bf16[128,2336]{0,1:T(8,128)(2,1)S(1)}, u32[]{:S(2)}, u32[]{:S(2)}) collective-permute-start(bf16[128,2336]{0,1:T(8,128)(2,1)S(1)} %copy.109), channel_id=1, source_target_pairs={{0,1},{1,0},{2,3},{3,2},{4,5},{5,4},{6,7},{7,6},{8,9},{9,8},{10,11... | collective-permute-start | bytes 1794056 | tf_op jit(solution)/shard_map/ppermute | solution.py:17
  123.8 50.4 %collective-permute-start.4 = (bf16[128,1024]{1,0:T(8,128)(2,1)S(1)}, bf16[128,1024]{1,0:T(8,128)(2,1)S(1)}, u32[]{:S(2)}, u32[]{:S(2)}) collective-permute-start(bf16[128,1024]{1,0:T(8,128)(2,1)S(1)} %convolution_convert_fusion.3), channel_id=1, source_target_pairs={{0,1},{1,0},{2,3},{3,2},{4,5},{5,4},{6,7},{7,6},{8,9},{9,8},{10,11... | collective-permute-start | bytes 786440 | tf_op jit(solution)/shard_map/ppermute | solution.py:17
  174.2 1.2 copy-start.2
where the time goes:
time: 177 us; the launch traced here: 176 us
  Pallas kernels  80.5 us (45%)
  waiting for transfers between devices  29.8 us (17%)
  matrix products  26.4 us (15%)
  local copies, waits for them, and re-layouts  19.7 us (11%)
  starting transfers between devices  10.1 us (6%)
  other arithmetic  8.71 us (5%)
    pallas_call x1, Pallas kernels, sum_shards(): pl.pallas_call(functools.partial(sum_kernel, seq, spans, tile), out_shape...  47.3 us
    pallas_call x1, Pallas kernels, scan_states(): pl.pallas_call(scan_kernel, out_shape=(state, state), in_specs=[pl.BlockS...  33.2 us
    ppermute x6, waiting for transfers between devices, shift(): lax.ppermute(value, axis, [(i, (i + step) % count) for i in range(count)])  29.8 us
    dot_general x11, matrix products, dot(): return lax.dot_general(a, b, (dims, ((), ())), preferred_element_type=F32)  11.5 us
    ppermute x6, starting transfers between devices, shift(): lax.ppermute(value, axis, [(i, (i + step) % count) for i in range(count)])  10.1 us
    dot_general x3, matrix products, bdot(): return jnp.einsum(spec, a, b, preferred_element_type=F32)  5.82 us
    unnamed x42, local copies, waits for them, and re-layouts  5.54 us
    dot_general x1, matrix products, per_device(): proj = jnp.dot(columns_of(here), w_in, preferred_element_type=F32)  4.08 us
  transfers between devices with their start and end apart: 6, of which 4 were waited for; matrix products, arithmetic and copies ran while one was open for 25% of the time, Pallas kernels for 46%

commit v1 on v0

--- a/solution.py
+++ b/solution.py
@@ -25,11 +25,13 @@
     return jnp.einsum(spec, a, b, preferred_element_type=F32)
 
 
-def greet(peers):
+def greet(peers, mates=()):
     barrier = pltpu.get_barrier_semaphore()
     for peer in peers:
         pl.semaphore_signal(barrier, inc=1, device_id={"seq": peer}, device_id_type=MESH)
-    pl.semaphore_wait(barrier, len(peers))
+    for mate in mates:
+        pl.semaphore_signal(barrier, inc=1, device_id={"zero": mate}, device_id_type=MESH)
+    pl.semaphore_wait(barrier, len(peers) + len(mates))
 
 
 def remote(src, dst, send, recv, peer):
@@ -163,53 +165,87 @@
     )(pair, totals)
 
 
-def sum_kernel(seq, spans, tile, left, right, out, *scratch):
+def tail_kernel(spans, tile, own, left, weights, out, grads, right, *scratch):
+    seq, zero = 2 * left.shape[1], left.shape[3] // own.shape[0]
     levels = (seq // 2).bit_length() - 1
-    me = lax.axis_index("seq")
+    me, here = lax.axis_index("seq"), lax.axis_index("zero")
     core, place = lax.rem(me, 2), lax.div(me, 2)
     bits = [lax.rem(lax.div(place, 1 << b), 2) for b in range(levels)]
     sibling = me + 1 - 2 * core
     partners = [me + (1 - 2 * bits[b]) * (2 << b) for b in range(levels)]
-    greet([sibling] + partners)
+    after = [lax.rem(here + s, zero) for s in range(zero)]
+    before = [lax.rem(here + zero - s, zero) for s in range(zero)]
+    greet([sibling] + partners, after[1:])
     pieces, piece, tokens = left.shape[1:]
+    count = own.shape[0]
     parts = len(spans)
     up = list(range(levels))
-    orders = [up, up[1:] + up[:1]] * (parts // 2)
+    orders = [up[1:] + up[:1]] + [up] * (parts - 1)
     acc, away, come = (scratch[i * parts : (i + 1) * parts] for i in range(3))
-    rest = scratch[3 * parts : -2]
+    rest = scratch[3 * parts : -7]
     outs = [rest[h * levels : (h + 1) * levels] for h in range(parts)]
     ins = [rest[(parts + h) * levels : (parts + h + 1) * levels] for h in range(parts)]
-    send, recv = scratch[-2:]
+    made, send, recv, put, got, leave, enter = scratch[-7:]
+
+    arriving = []
+    for h, (low, high) in enumerate(spans):
+        arriving.append([])
+        for s in range(1, zero):
+            copy = pltpu.make_async_remote_copy(
+                src_ref=own.at[:, low:high],
+                dst_ref=right.at[s * count : (s + 1) * count, low:high],
+                send_sem=put.at[h, s],
+                recv_sem=got.at[h, s],
+                device_id={"zero": after[s]},
+                device_id_type=MESH,
+            )
+            copy.start()
+            arriving[h].append(copy)
+    right[:count] = own[...]
+
+    owned = weights.shape[0]
+    base = pl.multiple_of(here * owned, 128)
+
+    def project(rows, target, first):
+        @pl.loop(0, owned // tile)
+        def _(i):
+            at = pl.multiple_of(i * tile, 128)
+            value = dot(rows[...], weights[pl.ds(at, tile)], ((1,), (1,)))
+            target[:, pl.ds(pl.multiple_of(first + at, 128), tile)] = value.astype(BF)
+
+    project(own, grads, base)
 
     def multiply(side, h, target):
         low, high = spans[h]
         rows = left[side].reshape(pieces * piece, tokens)
-        full = (high - low) // tile
-
-        def column(first, own, wide):
-            made = jnp.dot(rows, right[:, pl.ds(first, wide)], preferred_element_type=F32)
-            target[:, :, pl.ds(own, wide)] = made.reshape(pieces, piece, wide).astype(target.dtype)
-
-        @pl.loop(0, full)
-        def _(i):
-            own = pl.multiple_of(i * tile, 128)
-            column(pl.multiple_of(low + i * tile, 128), own, tile)
-
-        if (high - low) % tile:
-            column(low + full * tile, full * tile, (high - low) % tile)
+        value = jnp.dot(rows, right[:, low:high], preferred_element_type=F32)
+        target[...] = value.reshape(target.shape).astype(target.dtype)
 
     first = []
-    for h in range(parts):
+
+    def front(h):
+        for copy in arriving[h]:
+            copy.wait()
         multiply(1 - core, h, away[h])
         copy = remote(away[h], come[h], send.at[h, levels], recv.at[h, levels], sibling)
         copy.start()
         first.append(copy)
+        multiply(core, h, acc[h])
+
+    def join(h):
+        first[h].wait()
+
+        @pl.loop(0, pieces)
+        def _(i):
+            acc[h][i] += come[h][i].astype(F32)
 
     def subsets(rest):
         found = [0]
         for b in rest:
             found = found + [value + (1 << b) for value in found]
         return found
+
+    flying = {}
 
     def begin(h, s):
         order = orders[h]
@@ -219,57 +255,79 @@
             outs[h][s][j] = acc[h][base + (1 - bits[b]) * (1 << b) + extra].astype(BF)
         copy = remote(outs[h][s], ins[h][s], send.at[h, s], recv.at[h, s], partners[b])
         copy.start()
-        return copy
-
-    def finish(h, s, copy):
-        copy.wait()
+        flying[h] = copy
+
+    def finish(h, s):
+        flying[h].wait()
         order = orders[h]
         base = sum((bits[f] * (1 << f) for f in order[: s + 1]), 0)
         for j, extra in enumerate(subsets(order[s + 1 :])):
             acc[h][base + extra] += ins[h][s][j].astype(F32)
 
-    flying = []
-    for h in range(parts):
-        multiply(core, h, acc[h])
-        first[h].wait()
-
-        @pl.loop(0, pieces)
-        def _(i):
-            acc[h][i] += come[h][i].astype(F32)
-
-        flying.append(begin(h, 0))
-    for s in range(levels):
-        for h in range(parts):
-            finish(h, s, flying[h])
-            if s + 1 < levels:
-                flying[h] = begin(h, s + 1)
-    for h in range(parts):
-        out[:, spans[h][0] : spans[h][1]] = acc[h][place]
-
-
-def sum_shards(left, right):
-    pieces, piece = left.shape[1:3]
-    cols = right.shape[1]
-    seq = 2 * pieces
-    tile, parts = 384, 6
+    lag = 4
+    returning = []
+    for k in range(parts + lag + levels):
+        if k < parts:
+            front(k)
+        if 1 <= k <= parts:
+            join(k - 1)
+            begin(k - 1, 0)
+        if k == parts:
+            for s in range(1, zero):
+                project(right.at[s * count : (s + 1) * count], made.at[s - 1], 0)
+                copy = pltpu.make_async_remote_copy(
+                    src_ref=made.at[s - 1],
+                    dst_ref=grads.at[:, pl.ds(base, owned)],
+                    send_sem=leave.at[s],
+                    recv_sem=enter.at[s],
+                    device_id={"zero": before[s]},
+                    device_id_type=MESH,
+                )
+                copy.start()
+                returning.append(copy)
+        for s in reversed(range(levels)):
+            h = k - lag - s
+            if 0 <= h < parts:
+                finish(h, s)
+                if s + 1 < levels:
+                    begin(h, s + 1)
+                else:
+                    out[:, spans[h][0] : spans[h][1]] = acc[h][place]
+    for copy in returning:
+        copy.wait()
+
+
+def tail(own, left, weights):
+    pieces, piece, tokens = left.shape[1:]
+    count, cols = own.shape
+    zero = tokens // count
+    parts = max(2, cols // 256)
     levels = pieces.bit_length() - 1
-    edges = [(2 * i * cols // parts + 128) // 256 * 128 for i in range(parts)] + [cols]
+    edges = [i * cols // parts // 128 * 128 for i in range(parts)] + [cols]
     spans = list(zip(edges[:-1], edges[1:]))
     widths = [high - low for low, high in spans]
-    scratch = [pltpu.VMEM((pieces, piece, w), F32) for w in widths]
+    scratch = [pltpu.VMEM((tokens, cols), BF)]
+    scratch += [pltpu.VMEM((pieces, piece, w), F32) for w in widths]
     scratch += [pltpu.VMEM((pieces, piece, w), BF) for w in widths] * 2
     for _ in range(2):
         for w in widths:
             scratch += [pltpu.VMEM((pieces >> (s + 1), piece, w), BF) for s in range(levels)]
+    owned = weights.shape[0]
+    scratch += [pltpu.VMEM((zero - 1, count, owned), BF)]
     scratch += [pltpu.SemaphoreType.DMA((parts, levels + 1))] * 2
+    scratch += [pltpu.SemaphoreType.DMA((parts, zero))] * 2
+    scratch += [pltpu.SemaphoreType.DMA((zero,))] * 2
     return pl.pallas_call(
-        functools.partial(sum_kernel, seq, spans, tile),
-        out_shape=jax.ShapeDtypeStruct((piece, cols), F32),
-        in_specs=[pl.BlockSpec(memory_space=pltpu.VMEM)] * 2,
-        out_specs=pl.BlockSpec(memory_space=pltpu.VMEM),
+        functools.partial(tail_kernel, spans, min(256, owned)),
+        out_shape=(
+            jax.ShapeDtypeStruct((piece, cols), F32),
+            jax.ShapeDtypeStruct((count, zero * owned), BF),
+        ),
+        in_specs=[pl.BlockSpec(memory_space=pltpu.VMEM)] * 3,
+        out_specs=[pl.BlockSpec(memory_space=pltpu.VMEM)] * 2,
         scratch_shapes=scratch,
         compiler_params=pltpu.CompilerParams(collective_id=1, has_side_effects=True),
-    )(left, right)
+    )(own, left, weights)
 
 
 def ssd_block(proj, gy, a_log, dt_bias, d_skip):
@@ -373,23 +431,10 @@
 
     y_out, gproj = ssd_block(proj, grad_y.reshape(count, inner), a_log, dt_bias, d_skip)
 
-    others = [shift(gproj, "zero", s) for s in range(1, zero)]
-    mine = dot(gproj, w_in, ((1,), (1,))).astype(BF)
-    grads = [mine]
-    for s, other in zip(range(1, zero), others):
-        grads.append(shift(dot(other, w_in, ((1,), (1,))).astype(BF), "zero", zero - s))
-    blocks = []
-    for z in range(zero):
-        block = grads[0]
-        for s in range(1, zero):
-            block = jnp.where((here + s) % zero == z, grads[s], block)
-        blocks.append(block)
-    grad_tokens = jnp.concatenate(blocks, axis=1).reshape(1, count, width)
-
     left = jnp.concatenate([pieces_of(here)] + theirs, axis=0)
-    right = jnp.concatenate([gproj] + others, axis=0)
     left = left.reshape(left.shape[0], seq // 2, 2, piece).transpose(2, 1, 3, 0)
-    grad_w = sum_shards(left, right)
+    grad_w, grad_tokens = tail(gproj, left, w_in)
+    grad_tokens = grad_tokens.reshape(1, count, width)
     return (y_out.reshape(1, count, inner), grad_tokens, grad_w)
 
 

time: 177 us -> 176 us (level)
  Pallas kernels: 80.5 us -> 99.1 us
  waiting for transfers between devices: 29.8 us -> 14.4 us
  local copies, waits for them, and re-layouts: 19.7 us -> 25.6 us
  matrix products: 26.4 us -> 21.1 us
  starting transfers between devices: 10.1 us -> 6.96 us
    pallas_call x1, Pallas kernels: 47.3 us -> 65.8 us  [tail(): pl.pallas_call(functools.partial(tail_kernel, spans, min(256, owned)), ou...]
    ppermute x6 -> x4, waiting for transfers between devices: 29.8 us -> 14.4 us  [shift(): lax.ppermute(value, axis, [(i, (i + step) % count) for i in range(count)])]
    unnamed x42 -> x26, local copies, waits for them, and re-layouts: 5.54 us -> 15.2 us
    dot_general x11 -> x9, matrix products: 11.5 us -> 5.68 us  [dot(): return lax.dot_general(a, b, (dims, ((), ())), preferred_element_type=F32)]
    ppermute x6 -> x4, starting transfers between devices: 10.1 us -> 6.96 us  [shift(): lax.ppermute(value, axis, [(i, (i + step) % count) for i in range(count)])]
  transfers between devices with their start and end apart: 6 -> 4, of which waited for: 4 -> 2; matrix products, arithmetic and copies ran while one was open for 25% -> 6% of each run, Pallas kernels for 46% -> 0%
where the time goes in v1:
time: 176 us; the launch traced here: 175 us
  Pallas kernels  99.1 us (56%)
  local copies, waits for them, and re-layouts  25.6 us (15%)
  matrix products  21.1 us (12%)
  waiting for transfers between devices  14.4 us (8%)
  other arithmetic  7.02 us (4%)
  starting transfers between devices  6.96 us (4%)
    pallas_call x1, Pallas kernels, tail(): pl.pallas_call(functools.partial(tail_kernel, spans, min(256, owned)), ou...  65.8 us
    pallas_call x1, Pallas kernels, scan_states(): pl.pallas_call(scan_kernel, out_shape=(state, state), in_specs=[pl.BlockS...  33.3 us
    unnamed x26, local copies, waits for them, and re-layouts  15.2 us
    ppermute x4, waiting for transfers between devices, shift(): lax.ppermute(value, axis, [(i, (i + step) % count) for i in range(count)])  14.4 us
    ppermute x4, starting transfers between devices, shift(): lax.ppermute(value, axis, [(i, (i + step) % count) for i in range(count)])  6.96 us
    dot_general x3, matrix products, bdot(): return jnp.einsum(spec, a, b, preferred_element_type=F32)  6.31 us
    dot_general x9, matrix products, dot(): return lax.dot_general(a, b, (dims, ((), ())), preferred_element_type=F32)  5.68 us
    dot_general x1, matrix products, per_device(): proj = jnp.dot(columns_of(here), w_in, preferred_element_type=F32)  4.08 us
  transfers between devices with their start and end apart: 4, of which 2 were waited for; matrix products, arithmetic and copies ran while one was open for 6% of the time, Pallas kernels for 0%

profile of v1, /device:TPU:0, one launch (start us, length us, event | category | flops | bytes accessed | tf_op | source)
XLA Modules:
  0.0 175.1 jit_solution(17166058911690597080)
XLA Ops:
  0.6 1.0 dynamic-slice_bitcast_fusion
  1.6 3.1 %collective-permute-start = (bf16[128,1024]{1,0:T(8,128)(2,1)S(1)}, bf16[128,1024]{1,0:T(8,128)(2,1)S(1)}, u32[]{:S(2)}, u32[]{:S(2)}) collective-permute-start(bf16[128,1024]{1,0:T(8,128)(2,1)S(1)} %dynamic-slice_bitcast_fusion), channel_id=1, source_target_pairs={{0,1},{1,0},{2,3},{3,2},{4,5},{5,4},{6,7},{7,6},{8,9},{9,8},{10,11... | collective-permute-start | bytes 786440 | tf_op jit(solution)/shard_map/ppermute | solution.py:17
  4.7 6.3 %collective-permute-done = bf16[128,1024]{1,0:T(8,128)(2,1)S(1)} collective-permute-done((bf16[128,1024]{1,0:T(8,128)(2,1)S(1)}, bf16[128,1024]{1,0:T(8,128)(2,1)S(1)}, u32[]{:S(2)}, u32[]{:S(2)}) %collective-permute-start) | collective-permute-done | bytes 262176 | tf_op jit(solution)/shard_map/ppermute | solution.py:17
  11.0 3.8 %fusion.49 = f32[128,2336]{0,1:T(8,128)S(1)} fusion(bf16[128,1024]{1,0:T(8,128)(2,1)S(1)} %collective-permute-done, bf16[1024,2336]{0,1:T(8,128)(2,1)} %param.7), kind=kOutput, calls=%fused_computation.87 | convolution fusion | flops 612368384 | bytes 6242304 | tf_op jit(solution)/shard_map/dot_general | solution.py:419
  14.8 0.0 copy-start.2
  14.8 0.1 slice.73
  14.8 1.1 copy.127
  15.9 1.7 collective-permute-start.1
  17.6 0.3 copy.110
  18.0 0.3 collective-permute-start.3
  18.3 0.0 copy-start.7
  18.4 7.4 %copy.113.weights = bf16[1024,2336]{1,0:T(8,128)(2,1)} copy(bf16[1024,2336]{0,1:T(8,128)(2,1)} %param.7) | data formatting | bytes 9568256 | tf_op args[1]
  25.7 1.3 copy.100
  27.1 0.1 copy.128
  27.2 1.8 %collective-permute-start.2 = (f32[128,32]{1,0:T(8,128)S(1)}, f32[128,32]{1,0:T(8,128)S(1)}, u32[]{:S(2)}, u32[]{:S(2)}) collective-permute-start(f32[128,32]{1,0:T(8,128)S(1)} %copy.128), channel_id=1, source_target_pairs={{0,1},{1,0},{2,3},{3,2},{4,5},{5,4},{6,7},{7,6},{8,9},{9,8},{10,11... | collective-permute-start | bytes 49160 | tf_op jit(solution)/shard_map/ppermute | solution.py:17
  29.0 8.1 %collective-permute-done.3 = bf16[128,1024]{0,1:T(8,128)(2,1)} collective-permute-done((bf16[128,1024]{0,1:T(8,128)(2,1)S(1)}, bf16[128,1024]{0,1:T(8,128)(2,1)}, u32[]{:S(2)}, u32[]{:S(2)}) %collective-permute-start.3) | collective-permute-done | bytes 262176 | tf_op jit(solution)/shard_map/ppermute | solution.py:17
  37.0 1.8 %copy_bitcast_fusion.left = bf16[2,8,64,256]{3,2,1,0:T(8,128)(2,1)} fusion(bf16[128,8,2,64]{0,3,2,1:T(8,128)(2,1)} %bitcast.38, bf16[128,8,2,64]{0,3,2,1:T(8,128)(2,1)S(1)} %bitcast.113), kind=kLoop, calls=%fused_computation.48 | loop fusion | flops 1048576 | bytes 1048576 | tf_op jit(solution)/shard_map/transpose | solution.py:435
  38.9 0.0 collective-permute-done.1
  38.9 0.1 convert_element_type.101
  38.9 0.0 copy-start.6
  38.9 0.0 collective-permute-done.2
  39.0 4.1 %fusion.48 = (bf16[128,2336]{1,0:T(8,128)(2,1)S(1)}, f32[128,2336]{1,0:T(8,128)S(1)}) fusion(f32[128,32]{1,0:T(8,128)S(1)} %collective-permute-done.2, f32[128,2304]{1,0:T(8,128)S(1)} %convert_element_type.101, bf16[1024,2336]{0,1:T(8,128)(2,1)} %param.7, bf16[1,128,2048]{2,1,0:T(8,128)(2,1)S(1)} %copy-done.2, s32[]{:T(128)S(6)} %select_n.33), kind=kOutput, calls=%fused_computation.86 | convolution fusion | flops 613265408 | bytes 8085508 | tf_op jit(solution)/shard_map/dot_general | solution.py:417
  43.1 0.1 fusion.35
  43.2 1.3 slice_convert_fusion.1
  44.5 0.1 copy.93
  44.6 0.2 fusion.24
  44.8 0.2 slice_reduce_fusion
  45.0 0.1 copy.129
  45.1 0.1 reshape_squeeze.3
  45.1 0.1 subtract_exponential_fusion
  45.2 0.1 fusion.18
  45.4 0.3 fusion.4
  45.6 1.0 mul.147
  46.7 1.6 copy.98
  48.2 1.0 mul.139
  49.3 2.6 %copy.96 = f32[128,2048]{1,0:T(8,128)} copy(f32[128,2048]{0,1:T(8,128)} %bitcast.107) | data formatting | bytes 2097152 | tf_op jit(solution)/shard_map/mul | solution.py:351
  51.9 1.4 multiply_convert_fusion.1
  53.3 0.3 copy.99
  53.6 0.3 fusion.3
  53.9 1.1 pad_maximum_fusion.pair
  54.9 0.7 broadcast_in_dim.25.totals
  55.6 33.3 %shard_map.85 = (bf16[8,2,2,64,128]{4,3,2,1,0:T(8,128)(2,1)}, bf16[8,2,2,64,128]{4,3,2,1,0:T(8,128)(2,1)}) custom-call(bf16[8,2,2,2,64,128]{5,4,3,2,1,0:T(8,128)(2,1)} %pad_maximum_fusion.pair, f32[8,2,8,128]{3,2,1,0:T(8,128)} %broadcast_in_dim.25.totals), custom_call_target="tpu_custom_call" | custom-call | tf_op jit(solution)/shard_map/pallas_call | solution.py:144
  88.9 0.0 copy-start.5
  88.9 2.3 %fusion.28 = f32[128,32,64]{0,2,1:T(8,128)} fusion(bf16[32,64,128]{2,1,0:T(8,128)(2,1)} %bitcast.101, bf16[128,2336]{1,0:T(8,128)(2,1)S(1)} %get-tuple-element.37), kind=kOutput, calls=%fused_computation.60 | convolution fusion | flops 67108864 | bytes 1605632 | tf_op jit(solution)/shard_map/dot_general | solution.py:21
  91.2 1.5 copy.91
  92.8 3.3 %fusion.11 = (f32[128,32]{0,1:T(8,128)S(1)}, f32[128,32]{0,1:T(8,128)S(1)}, f32[32]{0:T(128)S(1)}, bf16[128,32,64]{0,2,1:T(8,128)(2,1)S(1)}, bf16[128,32,64]{0,2,1:T(8,128)(2,1)}) fusion(f32[128,2048]{0,1:T(8,128)S(1)} %copy.91, f32[128,32]{0,1:T(8,128)S(1)} %get-tuple-element.35, f32[128,32,64]{0,2,1:T(8,128)} %fusion.28, ...), kind=kOutput, calls=%fused_computation.29 | convolution fusion | flops 74178528 | bytes 4882688 | tf_op jit(solution)/shard_map/hts,thp->shp/dot_general | solution.py:25
  96.1 1.1 fusion
  97.2 1.9 %convolution_bitcast_fusion.1 = f32[128,32,64]{0,2,1:T(8,128)} fusion(bf16[128,32,64]{0,2,1:T(8,128)(2,1)S(1)} %get-tuple-element.26, f32[32,128]{1,0:T(8,128)S(1)} %bitcast.119, f32[128,128]{0,1:T(8,128)S(1)} %fusion.35, pred[128,128]{0,1:T(8,128)(4,1)S(1)} %iota_compare_fusion), kind=kOutput, calls=%fused_computation.11 | convolution fusion | flops 69730304 | bytes 1671168 | tf_op jit(solution)/shard_map/hts,shp->thp/dot_general | solution.py:25
  99.1 0.3 fusion.50
  99.4 0.3 multiply_reduce_fusion
  99.7 0.1 reduce_sum.65
  99.8 0.1 copy.108
  99.9 0.1 fusion.8
  100.0 1.8 fusion.17
  101.8 0.0 copy-start.4
  101.8 0.3 fusion.51
  102.1 0.2 fusion.9
  102.3 1.0 copy.114
  103.3 0.2 copy.109
  103.6 1.0 fusion.10
  104.6 0.9 pad_maximum_fusion.1.own
  105.5 65.8 %shard_map.86 = (f32[64,2336]{1,0:T(8,128)}, bf16[128,2048]{1,0:T(8,128)(2,1)}) custom-call(bf16[128,2336]{1,0:T(8,128)(2,1)} %pad_maximum_fusion.1.own, bf16[2,8,64,256]{3,2,1,0:T(8,128)(2,1)} %copy_bitcast_fusion.left, bf16[1024,2336]{1,0:T(8,128)(2,1)} %copy.113.weights), custom_call_target="tpu_custom_call" | custom-call | tf_op jit(solution)/shard_map/pallas_call | solution.py:320
  171.3 1.9 %copy.134 = bf16[1,128,2048]{2,1,0:T(8,128)(2,1)} copy(bf16[1,128,2048]{2,1,0:T(8,128)(2,1)} %bitcast.115) | data formatting | bytes 1048576
  173.2 1.9 %copy.135 = f32[64,2336]{1,0:T(8,128)} copy(f32[64,2336]{1,0:T(8,128)} %get-tuple-element.44) | data formatting | bytes 1196032
  (18 shorter events, 0.1 us)
Async XLA Ops:
  1.6 9.4 %collective-permute-start = (bf16[128,1024]{1,0:T(8,128)(2,1)S(1)}, bf16[128,1024]{1,0:T(8,128)(2,1)S(1)}, u32[]{:S(2)}, u32[]{:S(2)}) collective-permute-start(bf16[128,1024]{1,0:T(8,128)(2,1)S(1)} %dynamic-slice_bitcast_fusion), channel_id=1, source_target_pairs={{0,1},{1,0},{2,3},{3,2},{4,5},{5,4},{6,7},{7,6},{8,9},{9,8},{10,11... | collective-permute-start | bytes 786440 | tf_op jit(solution)/shard_map/ppermute | solution.py:17
  14.8 2.9 %copy-start.2 = (bf16[1,128,2048]{2,1,0:T(8,128)(2,1)S(1)}, bf16[1,128,2048]{2,1,0:T(8,128)(2,1)}, u32[]{:S(2)}) copy-start(bf16[1,128,2048]{2,1,0:T(8,128)(2,1)} %param.6) | copy-start | bytes 1572868
  15.9 23.0 %collective-permute-start.1 = (bf16[128,2304]{1,0:T(8,128)(2,1)}, bf16[128,2304]{1,0:T(8,128)(2,1)S(1)}, u32[]{:S(2)}, u32[]{:S(2)}) collective-permute-start(bf16[128,2304]{1,0:T(8,128)(2,1)} %copy.127), channel_id=1, source_target_pairs={{0,1},{1,0},{2,3},{3,2},{4,5},{5,4},{6,7},{7,6},{8,9},{9,8},{10,11... | collective-permute-start | bytes 1769480 | tf_op jit(solution)/shard_map/ppermute | solution.py:17
  18.0 19.1 %collective-permute-start.3 = (bf16[128,1024]{0,1:T(8,128)(2,1)S(1)}, bf16[128,1024]{0,1:T(8,128)(2,1)}, u32[]{:S(2)}, u32[]{:S(2)}) collective-permute-start(bf16[128,1024]{0,1:T(8,128)(2,1)S(1)} %bitcast.116), channel_id=1, source_target_pairs={{0,1},{1,0},{2,3},{3,2},{4,5},{5,4},{6,7},{7,6},{8,9},{9,8},{10,11... | collective-permute-start | bytes 786440 | tf_op jit(solution)/shard_map/ppermute | solution.py:17
  18.3 8.7 %copy-start.7 = (f32[32]{0:T(128)S(1)}, f32[32]{0:T(128)}, u32[]{:S(2)}) copy-start(f32[32]{0:T(128)} %param.8) | copy-start | bytes 388
  27.2 11.8 %collective-permute-start.2 = (f32[128,32]{1,0:T(8,128)S(1)}, f32[128,32]{1,0:T(8,128)S(1)}, u32[]{:S(2)}, u32[]{:S(2)}) collective-permute-start(f32[128,32]{1,0:T(8,128)S(1)} %copy.128), channel_id=1, source_target_pairs={{0,1},{1,0},{2,3},{3,2},{4,5},{5,4},{6,7},{7,6},{8,9},{9,8},{10,11... | collective-permute-start | bytes 49160 | tf_op jit(solution)/shard_map/ppermute | solution.py:17
  38.9 5.5 %copy-start.6 = (f32[32]{0:T(128)S(1)}, f32[32]{0:T(128)}, u32[]{:S(2)}) copy-start(f32[32]{0:T(128)} %param.9) | copy-start | bytes 388
  43.0 1.4 copy-start.3
  88.9 3.9 %copy-start.5 = (f32[32]{0:T(128)S(1)}, f32[32]{0:T(128)}, u32[]{:S(2)}) copy-start(f32[32]{0:T(128)} %param.10) | copy-start | bytes 388
  97.2 1.9 %copy-start.1 = (bf16[8,2,2,64,128]{4,3,2,1,0:T(8,128)(2,1)S(1)}, bf16[8,2,2,64,128]{4,3,2,1,0:T(8,128)(2,1)}, u32[]{:S(2)}) copy-start(bf16[8,2,2,64,128]{4,3,2,1,0:T(8,128)(2,1)} %get-tuple-element.8) | copy-start | bytes 1572868
  97.2 2.2 %copy-start = (bf16[8,2,2,64,128]{4,3,2,1,0:T(8,128)(2,1)S(1)}, bf16[8,2,2,64,128]{4,3,2,1,0:T(8,128)(2,1)}, u32[]{:S(2)}) copy-start(bf16[8,2,2,64,128]{4,3,2,1,0:T(8,128)(2,1)} %get-tuple-element.7) | copy-start | bytes 1572868
  101.8 1.6 copy-start.4

commit v2 on v1

--- a/solution.py
+++ b/solution.py
@@ -203,14 +203,14 @@
             arriving[h].append(copy)
     right[:count] = own[...]
 
-    owned = weights.shape[0]
+    owned, columns = weights.shape
     base = pl.multiple_of(here * owned, 128)
 
     def project(rows, target, first):
         @pl.loop(0, owned // tile)
         def _(i):
             at = pl.multiple_of(i * tile, 128)
-            value = dot(rows[...], weights[pl.ds(at, tile)], ((1,), (1,)))
+            value = dot(rows[:, :columns], weights[pl.ds(at, tile)], ((1,), (1,)))
             target[:, pl.ds(pl.multiple_of(first + at, 128), tile)] = value.astype(BF)
 
     project(own, grads, base)
@@ -264,9 +264,9 @@
         for j, extra in enumerate(subsets(order[s + 1 :])):
             acc[h][base + extra] += ins[h][s][j].astype(F32)
 
-    lag = 4
+    lag, skew = 4, 2
     returning = []
-    for k in range(parts + lag + levels):
+    for k in range(parts + lag + skew * levels):
         if k < parts:
             front(k)
         if 1 <= k <= parts:
@@ -286,13 +286,14 @@
                 copy.start()
                 returning.append(copy)
         for s in reversed(range(levels)):
-            h = k - lag - s
+            h = k - lag - skew * s
             if 0 <= h < parts:
                 finish(h, s)
                 if s + 1 < levels:
                     begin(h, s + 1)
                 else:
-                    out[:, spans[h][0] : spans[h][1]] = acc[h][place]
+                    low, high = spans[h][0], min(spans[h][1], columns)
+                    out[:, low:high] = acc[h][place, :, : high - low]
     for copy in returning:
         copy.wait()
 
@@ -301,10 +302,10 @@
     pieces, piece, tokens = left.shape[1:]
     count, cols = own.shape
     zero = tokens // count
-    parts = max(2, cols // 256)
     levels = pieces.bit_length() - 1
-    edges = [i * cols // parts // 128 * 128 for i in range(parts)] + [cols]
+    edges = list(range(0, cols, 256)) + [cols]
     spans = list(zip(edges[:-1], edges[1:]))
+    parts = len(spans)
     widths = [high - low for low, high in spans]
     scratch = [pltpu.VMEM((tokens, cols), BF)]
     scratch += [pltpu.VMEM((pieces, piece, w), F32) for w in widths]
@@ -312,7 +313,7 @@
     for _ in range(2):
         for w in widths:
             scratch += [pltpu.VMEM((pieces >> (s + 1), piece, w), BF) for s in range(levels)]
-    owned = weights.shape[0]
+    owned, columns = weights.shape
     scratch += [pltpu.VMEM((zero - 1, count, owned), BF)]
     scratch += [pltpu.SemaphoreType.DMA((parts, levels + 1))] * 2
     scratch += [pltpu.SemaphoreType.DMA((parts, zero))] * 2
@@ -320,7 +321,7 @@
     return pl.pallas_call(
         functools.partial(tail_kernel, spans, min(256, owned)),
         out_shape=(
-            jax.ShapeDtypeStruct((piece, cols), F32),
+            jax.ShapeDtypeStruct((piece, columns), F32),
             jax.ShapeDtypeStruct((count, zero * owned), BF),
         ),
         in_specs=[pl.BlockSpec(memory_space=pltpu.VMEM)] * 3,
@@ -393,7 +394,14 @@
     ) + last
     grad_raw = (grad_dt + grad_log * rate) * jax.nn.sigmoid(raw)
     gproj = jnp.concatenate(
-        [grad_x.reshape(count, inner), grad_b, grad_c, grad_raw], axis=1
+        [
+            grad_x.reshape(count, inner),
+            grad_b,
+            grad_c,
+            grad_raw,
+            jnp.zeros((count, -proj.shape[1] % 128), F32),
+        ],
+        axis=1,
     ).astype(BF)
     return out.reshape(count, inner).astype(BF), gproj
 

time: 176 us -> 166 us (0.943)
  Pallas kernels: 99.1 us -> 88.7 us
    pallas_call x1, Pallas kernels: 65.8 us -> 55.4 us  [tail(): pl.pallas_call(functools.partial(tail_kernel, spans, min(256, owned)), ou...]
  transfers between devices with their start and end apart: 4 -> 4, of which waited for: 2 -> 2; matrix products, arithmetic and copies ran while one was open for 6% -> 7% of each run, Pallas kernels for 0% -> 0%
where the time goes in v2:
time: 166 us; the launch traced here: 165 us
  Pallas kernels  88.7 us (53%)
  local copies, waits for them, and re-layouts  26.6 us (16%)
  matrix products  21.1 us (13%)
  waiting for transfers between devices  14.4 us (9%)
  starting transfers between devices  6.96 us (4%)
  other arithmetic  6.15 us (4%)
    pallas_call x1, Pallas kernels, tail(): pl.pallas_call(functools.partial(tail_kernel, spans, min(256, owned)), ou...  55.4 us
    pallas_call x1, Pallas kernels, scan_states(): pl.pallas_call(scan_kernel, out_shape=(state, state), in_specs=[pl.BlockS...  33.3 us
    unnamed x26, local copies, waits for them, and re-layouts  15.2 us
    ppermute x4, waiting for transfers between devices, shift(): lax.ppermute(value, axis, [(i, (i + step) % count) for i in range(count)])  14.4 us
    ppermute x4, starting transfers between devices, shift(): lax.ppermute(value, axis, [(i, (i + step) % count) for i in range(count)])  6.96 us
    dot_general x3, matrix products, bdot(): return jnp.einsum(spec, a, b, preferred_element_type=F32)  6.31 us
    dot_general x9, matrix products, dot(): return lax.dot_general(a, b, (dims, ((), ())), preferred_element_type=F32)  5.68 us
    dot_general x1, matrix products, per_device(): proj = jnp.dot(columns_of(here), w_in, preferred_element_type=F32)  4.08 us
  transfers between devices with their start and end apart: 4, of which 2 were waited for; matrix products, arithmetic and copies ran while one was open for 7% of the time, Pallas kernels for 0%

profile of v2, /device:TPU:0, one launch (start us, length us, event | category | flops | bytes accessed | tf_op | source)
XLA Modules:
  0.0 164.8 jit_solution(1004279505974774117)
XLA Ops:
  0.6 1.0 dynamic-slice_bitcast_fusion
  1.6 3.1 %collective-permute-start = (bf16[128,1024]{1,0:T(8,128)(2,1)S(1)}, bf16[128,1024]{1,0:T(8,128)(2,1)S(1)}, u32[]{:S(2)}, u32[]{:S(2)}) collective-permute-start(bf16[128,1024]{1,0:T(8,128)(2,1)S(1)} %dynamic-slice_bitcast_fusion), channel_id=1, source_target_pairs={{0,1},{1,0},{2,3},{3,2},{4,5},{5,4},{6,7},{7,6},{8,9},{9,8},{10,11... | collective-permute-start | bytes 786440 | tf_op jit(solution)/shard_map/ppermute | solution.py:17
  4.7 6.3 %collective-permute-done = bf16[128,1024]{1,0:T(8,128)(2,1)S(1)} collective-permute-done((bf16[128,1024]{1,0:T(8,128)(2,1)S(1)}, bf16[128,1024]{1,0:T(8,128)(2,1)S(1)}, u32[]{:S(2)}, u32[]{:S(2)}) %collective-permute-start) | collective-permute-done | bytes 262176 | tf_op jit(solution)/shard_map/ppermute | solution.py:17
  11.0 3.8 %fusion.49 = f32[128,2336]{0,1:T(8,128)S(1)} fusion(bf16[128,1024]{1,0:T(8,128)(2,1)S(1)} %collective-permute-done, bf16[1024,2336]{0,1:T(8,128)(2,1)} %param.7), kind=kOutput, calls=%fused_computation.86 | convolution fusion | flops 612368384 | bytes 6242304 | tf_op jit(solution)/shard_map/dot_general | solution.py:427
  14.8 0.0 copy-start.2
  14.8 0.1 slice.73
  14.8 1.1 copy.127
  15.9 1.7 %collective-permute-start.1 = (bf16[128,2304]{1,0:T(8,128)(2,1)}, bf16[128,2304]{1,0:T(8,128)(2,1)S(1)}, u32[]{:S(2)}, u32[]{:S(2)}) collective-permute-start(bf16[128,2304]{1,0:T(8,128)(2,1)} %copy.127), channel_id=1, source_target_pairs={{0,1},{1,0},{2,3},{3,2},{4,5},{5,4},{6,7},{7,6},{8,9},{9,8},{10,11... | collective-permute-start | bytes 1769480 | tf_op jit(solution)/shard_map/ppermute | solution.py:17
  17.6 0.3 copy.110
  18.0 0.3 collective-permute-start.3
  18.3 0.0 copy-start.7
  18.4 7.4 %copy.113.weights = bf16[1024,2336]{1,0:T(8,128)(2,1)} copy(bf16[1024,2336]{0,1:T(8,128)(2,1)} %param.7) | data formatting | bytes 9568256 | tf_op args[1]
  25.7 1.3 copy.100
  27.1 0.1 copy.128
  27.2 1.8 %collective-permute-start.2 = (f32[128,32]{1,0:T(8,128)S(1)}, f32[128,32]{1,0:T(8,128)S(1)}, u32[]{:S(2)}, u32[]{:S(2)}) collective-permute-start(f32[128,32]{1,0:T(8,128)S(1)} %copy.128), channel_id=1, source_target_pairs={{0,1},{1,0},{2,3},{3,2},{4,5},{5,4},{6,7},{7,6},{8,9},{9,8},{10,11... | collective-permute-start | bytes 49160 | tf_op jit(solution)/shard_map/ppermute | solution.py:17
  29.0 8.1 %collective-permute-done.3 = bf16[128,1024]{0,1:T(8,128)(2,1)} collective-permute-done((bf16[128,1024]{0,1:T(8,128)(2,1)S(1)}, bf16[128,1024]{0,1:T(8,128)(2,1)}, u32[]{:S(2)}, u32[]{:S(2)}) %collective-permute-start.3) | collective-permute-done | bytes 262176 | tf_op jit(solution)/shard_map/ppermute | solution.py:17
  37.0 1.8 %copy_bitcast_fusion.left = bf16[2,8,64,256]{3,2,1,0:T(8,128)(2,1)} fusion(bf16[128,8,2,64]{0,3,2,1:T(8,128)(2,1)} %bitcast.38, bf16[128,8,2,64]{0,3,2,1:T(8,128)(2,1)S(1)} %bitcast.113), kind=kLoop, calls=%fused_computation.47 | loop fusion | flops 1048576 | bytes 1048576 | tf_op jit(solution)/shard_map/transpose | solution.py:443
  38.9 0.0 collective-permute-done.1
  38.9 0.1 convert_element_type.101
  38.9 0.0 copy-start.6
  38.9 0.0 collective-permute-done.2
  39.0 4.1 %fusion.48 = (bf16[128,2336]{1,0:T(8,128)(2,1)S(1)}, f32[128,2336]{1,0:T(8,128)S(1)}) fusion(f32[128,32]{1,0:T(8,128)S(1)} %collective-permute-done.2, f32[128,2304]{1,0:T(8,128)S(1)} %convert_element_type.101, bf16[1024,2336]{0,1:T(8,128)(2,1)} %param.7, bf16[1,128,2048]{2,1,0:T(8,128)(2,1)S(1)} %copy-done.2, s32[]{:T(128)S(6)} %select_n.33), kind=kOutput, calls=%fused_computation.85 | convolution fusion | flops 613265408 | bytes 8085508 | tf_op jit(solution)/shard_map/dot_general | solution.py:425
  43.1 0.1 fusion.35
  43.2 1.3 slice_convert_fusion.1
  44.5 0.1 copy.93
  44.6 0.2 fusion.24
  44.8 0.2 slice_reduce_fusion
  45.0 0.1 copy.129
  45.1 0.1 reshape_squeeze.3
  45.1 0.1 subtract_exponential_fusion
  45.2 0.1 fusion.18
  45.4 0.3 fusion.4
  45.6 1.0 mul.147
  46.7 1.6 copy.98
  48.2 1.0 mul.139
  49.3 2.6 %copy.96 = f32[128,2048]{1,0:T(8,128)} copy(f32[128,2048]{0,1:T(8,128)} %bitcast.107) | data formatting | bytes 2097152 | tf_op jit(solution)/shard_map/mul | solution.py:352
  51.9 1.4 multiply_convert_fusion.1
  53.3 0.3 copy.99
  53.6 0.3 fusion.3
  53.9 1.1 pad_maximum_fusion.pair
  54.9 0.7 broadcast_in_dim.27.totals
  55.6 33.3 %shard_map.85 = (bf16[8,2,2,64,128]{4,3,2,1,0:T(8,128)(2,1)}, bf16[8,2,2,64,128]{4,3,2,1,0:T(8,128)(2,1)}) custom-call(bf16[8,2,2,2,64,128]{5,4,3,2,1,0:T(8,128)(2,1)} %pad_maximum_fusion.pair, f32[8,2,8,128]{3,2,1,0:T(8,128)} %broadcast_in_dim.27.totals), custom_call_target="tpu_custom_call" | custom-call | tf_op jit(solution)/shard_map/pallas_call | solution.py:144
  88.9 0.0 copy-start.5
  88.9 2.3 %fusion.28 = f32[128,32,64]{0,2,1:T(8,128)} fusion(bf16[32,64,128]{2,1,0:T(8,128)(2,1)} %bitcast.101, bf16[128,2336]{1,0:T(8,128)(2,1)S(1)} %get-tuple-element.37), kind=kOutput, calls=%fused_computation.59 | convolution fusion | flops 67108864 | bytes 1605632 | tf_op jit(solution)/shard_map/dot_general | solution.py:21
  91.2 1.5 copy.91
  92.8 3.3 %fusion.11 = (f32[128,32]{0,1:T(8,128)S(1)}, f32[128,32]{0,1:T(8,128)S(1)}, f32[32]{0:T(128)S(1)}, bf16[128,32,64]{0,2,1:T(8,128)(2,1)S(1)}, bf16[128,32,64]{0,2,1:T(8,128)(2,1)}) fusion(f32[128,2048]{0,1:T(8,128)S(1)} %copy.91, f32[128,32]{0,1:T(8,128)S(1)} %get-tuple-element.35, f32[128,32,64]{0,2,1:T(8,128)} %fusion.28, ...), kind=kOutput, calls=%fused_computation.29 | convolution fusion | flops 74178528 | bytes 4882688 | tf_op jit(solution)/shard_map/hts,thp->shp/dot_general | solution.py:25
  96.1 1.1 fusion
  97.2 1.9 %convolution_bitcast_fusion.1 = f32[128,32,64]{0,2,1:T(8,128)} fusion(bf16[128,32,64]{0,2,1:T(8,128)(2,1)S(1)} %get-tuple-element.26, f32[32,128]{1,0:T(8,128)S(1)} %bitcast.119, f32[128,128]{0,1:T(8,128)S(1)} %fusion.35, pred[128,128]{0,1:T(8,128)(4,1)S(1)} %iota_compare_fusion), kind=kOutput, calls=%fused_computation.11 | convolution fusion | flops 69730304 | bytes 1671168 | tf_op jit(solution)/shard_map/hts,shp->thp/dot_general | solution.py:25
  99.1 0.3 fusion.50
  99.4 0.3 multiply_reduce_fusion
  99.7 0.1 reduce_sum.65
  99.8 0.1 copy.108
  99.9 0.1 fusion.8
  100.0 1.8 %fusion.17 = (f32[128,32]{0,1:T(8,128)S(1)}, bf16[128,32,64]{0,2,1:T(8,128)(2,1)S(1)}, bf16[128,32,64]{0,2,1:T(8,128)(2,1)S(1)}) fusion(bf16[128,32,64]{0,2,1:T(8,128)(2,1)S(1)} %bitcast.98, f32[128,32,64]{0,2,1:T(8,128)S(1)} %bitcast.105, f32[32]{0:T(128)S(1)} %copy-done.5, f32[128,32]{0,1:T(8,128)S(1)} %get-tuple-element.36, ...), kind=kOutput, calls=%fused_computation.35 | convolution fusion | flops 69726208 | bytes 4260352 | tf_op jit(solution)/shard_map/dot_general | solution.py:21
  101.8 0.0 copy-start.4
  101.8 0.3 fusion.51
  102.1 0.2 fusion.9
  102.3 1.0 copy.114
  103.3 0.2 copy.109
  103.6 1.0 fusion.10
  104.6 1.0 concatenate.18.own
  105.6 55.4 %shard_map.86 = (f32[64,2336]{1,0:T(8,128)}, bf16[128,2048]{1,0:T(8,128)(2,1)}) custom-call(bf16[128,2432]{1,0:T(8,128)(2,1)} %concatenate.18.own, bf16[2,8,64,256]{3,2,1,0:T(8,128)(2,1)} %copy_bitcast_fusion.left, bf16[1024,2336]{1,0:T(8,128)(2,1)} %copy.113.weights), custom_call_target="tpu_custom_call" | custom-call | tf_op jit(solution)/shard_map/pallas_call | solution.py:321
  161.0 1.9 %copy.134 = bf16[1,128,2048]{2,1,0:T(8,128)(2,1)} copy(bf16[1,128,2048]{2,1,0:T(8,128)(2,1)} %bitcast.115) | data formatting | bytes 1048576
  162.9 1.9 %copy.135 = f32[64,2336]{1,0:T(8,128)} copy(f32[64,2336]{1,0:T(8,128)} %get-tuple-element.44) | data formatting | bytes 1196032
  (19 shorter events, 0.2 us)
Async XLA Ops:
  1.6 9.4 %collective-permute-start = (bf16[128,1024]{1,0:T(8,128)(2,1)S(1)}, bf16[128,1024]{1,0:T(8,128)(2,1)S(1)}, u32[]{:S(2)}, u32[]{:S(2)}) collective-permute-start(bf16[128,1024]{1,0:T(8,128)(2,1)S(1)} %dynamic-slice_bitcast_fusion), channel_id=1, source_target_pairs={{0,1},{1,0},{2,3},{3,2},{4,5},{5,4},{6,7},{7,6},{8,9},{9,8},{10,11... | collective-permute-start | bytes 786440 | tf_op jit(solution)/shard_map/ppermute | solution.py:17
  14.8 2.9 %copy-start.2 = (bf16[1,128,2048]{2,1,0:T(8,128)(2,1)S(1)}, bf16[1,128,2048]{2,1,0:T(8,128)(2,1)}, u32[]{:S(2)}) copy-start(bf16[1,128,2048]{2,1,0:T(8,128)(2,1)} %param.6) | copy-start | bytes 1572868
  15.9 23.0 %collective-permute-start.1 = (bf16[128,2304]{1,0:T(8,128)(2,1)}, bf16[128,2304]{1,0:T(8,128)(2,1)S(1)}, u32[]{:S(2)}, u32[]{:S(2)}) collective-permute-start(bf16[128,2304]{1,0:T(8,128)(2,1)} %copy.127), channel_id=1, source_target_pairs={{0,1},{1,0},{2,3},{3,2},{4,5},{5,4},{6,7},{7,6},{8,9},{9,8},{10,11... | collective-permute-start | bytes 1769480 | tf_op jit(solution)/shard_map/ppermute | solution.py:17
  18.0 19.1 %collective-permute-start.3 = (bf16[128,1024]{0,1:T(8,128)(2,1)S(1)}, bf16[128,1024]{0,1:T(8,128)(2,1)}, u32[]{:S(2)}, u32[]{:S(2)}) collective-permute-start(bf16[128,1024]{0,1:T(8,128)(2,1)S(1)} %bitcast.116), channel_id=1, source_target_pairs={{0,1},{1,0},{2,3},{3,2},{4,5},{5,4},{6,7},{7,6},{8,9},{9,8},{10,11... | collective-permute-start | bytes 786440 | tf_op jit(solution)/shard_map/ppermute | solution.py:17
  18.3 8.7 %copy-start.7 = (f32[32]{0:T(128)S(1)}, f32[32]{0:T(128)}, u32[]{:S(2)}) copy-start(f32[32]{0:T(128)} %param.8) | copy-start | bytes 388
  27.2 11.8 %collective-permute-start.2 = (f32[128,32]{1,0:T(8,128)S(1)}, f32[128,32]{1,0:T(8,128)S(1)}, u32[]{:S(2)}, u32[]{:S(2)}) collective-permute-start(f32[128,32]{1,0:T(8,128)S(1)} %copy.128), channel_id=1, source_target_pairs={{0,1},{1,0},{2,3},{3,2},{4,5},{5,4},{6,7},{7,6},{8,9},{9,8},{10,11... | collective-permute-start | bytes 49160 | tf_op jit(solution)/shard_map/ppermute | solution.py:17
  38.9 5.5 %copy-start.6 = (f32[32]{0:T(128)S(1)}, f32[32]{0:T(128)}, u32[]{:S(2)}) copy-start(f32[32]{0:T(128)} %param.9) | copy-start | bytes 388
  43.0 1.4 copy-start.3
  88.9 3.9 %copy-start.5 = (f32[32]{0:T(128)S(1)}, f32[32]{0:T(128)}, u32[]{:S(2)}) copy-start(f32[32]{0:T(128)} %param.10) | copy-start | bytes 388
  97.2 1.9 %copy-start.1 = (bf16[8,2,2,64,128]{4,3,2,1,0:T(8,128)(2,1)S(1)}, bf16[8,2,2,64,128]{4,3,2,1,0:T(8,128)(2,1)}, u32[]{:S(2)}) copy-start(bf16[8,2,2,64,128]{4,3,2,1,0:T(8,128)(2,1)} %get-tuple-element.8) | copy-start | bytes 1572868
  97.2 2.2 %copy-start = (bf16[8,2,2,64,128]{4,3,2,1,0:T(8,128)(2,1)S(1)}, bf16[8,2,2,64,128]{4,3,2,1,0:T(8,128)(2,1)}, u32[]{:S(2)}) copy-start(bf16[8,2,2,64,128]{4,3,2,1,0:T(8,128)(2,1)} %get-tuple-element.7) | copy-start | bytes 1572868
  101.8 1.6 copy-start.4

commit v3 on v2

--- a/solution.py
+++ b/solution.py
@@ -45,9 +45,115 @@
     )
 
 
+def mate(src, dst, send, recv, peer):
+    return pltpu.make_async_remote_copy(
+        src_ref=src,
+        dst_ref=dst,
+        send_sem=send,
+        recv_sem=recv,
+        device_id={"zero": peer},
+        device_id_type=MESH,
+    )
+
+
+def head_kernel(
+    zero, inner, rows, stored, xs, pair, raw, weights, guest, kept, made, narrow, back, thin,
+    send, recv, load
+):
+    here = lax.axis_index("zero")
+    columns, owned = weights.shape
+    exact = made.shape[2]
+    heads = columns - exact
+    after = [lax.rem(here + s, zero) for s in range(zero)]
+    before = [lax.rem(here + zero - s, zero) for s in range(zero)]
+    fetch = pltpu.make_async_copy(stored, weights, load)
+    fetch.start()
+    greet([], after[1:])
+
+    def columns_of(z):
+        return pl.ds(pl.multiple_of(z * owned, 128), owned)
+
+    coming = []
+    for s in range(1, zero):
+        copy = mate(rows.at[:, columns_of(after[s])], guest.at[s - 1], send.at[s, 0], recv.at[s, 0], after[s])
+        copy.start()
+        coming.append(copy)
+    edges = list(range(0, inner, 256)) + [inner]
+    spans = [(inner, exact)] + list(zip(edges[:-1], edges[1:]))
+    fetch.wait()
+    mine = rows[:, columns_of(here)]
+    for low, high in spans + [(exact, columns)]:
+        kept[:, low:high] = dot(mine, weights[low:high], ((1,), (1,)))
+    going = {}
+    narrow[...] = jnp.zeros(narrow.shape, F32)
+    for s in range(1, zero):
+        coming[s - 1].wait()
+        narrow[s - 1, :, :heads] = dot(guest[s - 1], weights[exact:], ((1,), (1,)))
+        copy = mate(narrow.at[s - 1], thin.at[s - 1], send.at[s, 1], recv.at[s, 1], before[s])
+        copy.start()
+        going[s, -1] = copy
+        for i, (low, high) in enumerate(spans):
+            value = dot(guest[s - 1], weights[low:high], ((1,), (1,)))
+            made[s - 1, :, low:high] = value.astype(BF)
+            copy = mate(
+                made.at[s - 1, :, low:high],
+                back.at[s - 1, :, low:high],
+                send.at[s, 2 + i],
+                recv.at[s, 2 + i],
+                before[s],
+            )
+            copy.start()
+            going[s, i] = copy
+    total = kept[:, exact:]
+    for s in range(1, zero):
+        going[s, -1].wait()
+        total = total + thin[s - 1, :, :heads]
+    raw[...] = total
+    for i, (low, high) in enumerate(spans):
+        total = kept[:, low:high]
+        for s in range(1, zero):
+            going[s, i].wait()
+            total = total + back[s - 1, :, low:high].astype(F32)
+        if i:
+            xs[:, low:high] = total.astype(BF)
+        else:
+            pair[...] = total.astype(BF)
+
+
+def head(rows, weights, inner, heads):
+    count, width = rows.shape
+    columns, owned = weights.shape
+    zero = width // owned
+    exact = columns - heads
+    steps = 3 + -(-inner // 256)
+    return pl.pallas_call(
+        functools.partial(head_kernel, zero, inner),
+        out_shape=(
+            jax.ShapeDtypeStruct((count, inner), BF),
+            jax.ShapeDtypeStruct((count, exact - inner), BF),
+            jax.ShapeDtypeStruct((count, heads), F32),
+        ),
+        in_specs=[pl.BlockSpec(memory_space=pltpu.VMEM), pl.BlockSpec(memory_space=pl.ANY)],
+        out_specs=[pl.BlockSpec(memory_space=pltpu.VMEM)] * 3,
+        scratch_shapes=[
+            pltpu.VMEM((columns, owned), BF),
+            pltpu.VMEM((zero - 1, count, owned), BF),
+            pltpu.VMEM((count, columns), F32),
+            pltpu.VMEM((zero - 1, count, exact), BF),
+            pltpu.VMEM((zero - 1, count, 128), F32),
+            pltpu.VMEM((zero - 1, count, exact), BF),
+            pltpu.VMEM((zero - 1, count, 128), F32),
+            pltpu.SemaphoreType.DMA((zero, steps)),
+            pltpu.SemaphoreType.DMA((zero, steps)),
+            pltpu.SemaphoreType.DMA,
+        ],
+        compiler_params=pltpu.CompilerParams(collective_id=2, has_side_effects=True),
+    )(rows, weights)
+
+
 def scan_kernel(
-    pair, totals, start, end, both, marks, joined, sums, got, lengths, made, back, final, wide,
-    send, recv, local
+    pair, totals, guests, start, end, held, both, marks, joined, sums, got, lengths, made, back, final, wide,
+    send, recv, local, leave, enter
 ):
     chips, _, share = pair.shape[:3]
     me = lax.axis_index("seq")
@@ -55,7 +161,16 @@
     sibling = me + 1 - 2 * core
     places = [lax.rem(chip + d, chips) for d in range(1, chips)]
     peers = [place * 2 + core for place in places]
-    greet([sibling] + peers)
+    here = lax.axis_index("zero")
+    zero = guests.shape[0] + 1
+    after = [lax.rem(here + s, zero) for s in range(zero)]
+    greet([sibling] + peers, after[1:])
+    crossing = [
+        mate(guests.at[s - 1], held.at[s - 1], leave.at[s - 1], enter.at[s - 1], after[s])
+        for s in range(1, zero)
+    ]
+    for copy in crossing:
+        copy.start()
 
     def move(copies):
         for copy in copies:
@@ -134,18 +249,20 @@
     for parity in range(2):
         start[:, parity] = wide[parity, :, :, 0]
         end[:, parity] = wide[parity, :, :, 1]
-
-
-def scan_states(pair, totals):
+    for copy in crossing:
+        copy.wait()
+
+
+def scan_states(pair, totals, guests):
     chips, _, share, _, rows, lanes = pair.shape
     state = jax.ShapeDtypeStruct((chips, 2, share, rows, lanes), BF)
     half = (chips,) + pair.shape[2:]
     short = (chips,) + totals.shape[2:]
     return pl.pallas_call(
         scan_kernel,
-        out_shape=(state, state),
-        in_specs=[pl.BlockSpec(memory_space=pltpu.VMEM)] * 2,
-        out_specs=[pl.BlockSpec(memory_space=pltpu.VMEM)] * 2,
+        out_shape=(state, state, jax.ShapeDtypeStruct(guests.shape, BF)),
+        in_specs=[pl.BlockSpec(memory_space=pltpu.VMEM)] * 3,
+        out_specs=[pl.BlockSpec(memory_space=pltpu.VMEM)] * 3,
         scratch_shapes=[
             pltpu.VMEM((2,) + half, BF),
             pltpu.VMEM((2,) + short, F32),
@@ -160,12 +277,14 @@
             pltpu.SemaphoreType.DMA((6, chips)),
             pltpu.SemaphoreType.DMA((6, chips)),
             pltpu.SemaphoreType.DMA((6,)),
+            pltpu.SemaphoreType.DMA(guests.shape[:1]),
+            pltpu.SemaphoreType.DMA(guests.shape[:1]),
         ],
         compiler_params=pltpu.CompilerParams(collective_id=0, has_side_effects=True),
-    )(pair, totals)
-
-
-def tail_kernel(spans, tile, own, left, weights, out, grads, right, *scratch):
+    )(pair, totals, guests)
+
+
+def tail_kernel(spans, tile, own, left, stored, out, grads, right, weights, *scratch):
     seq, zero = 2 * left.shape[1], left.shape[3] // own.shape[0]
     levels = (seq // 2).bit_length() - 1
     me, here = lax.axis_index("seq"), lax.axis_index("zero")
@@ -175,6 +294,9 @@
     partners = [me + (1 - 2 * bits[b]) * (2 << b) for b in range(levels)]
     after = [lax.rem(here + s, zero) for s in range(zero)]
     before = [lax.rem(here + zero - s, zero) for s in range(zero)]
+    load = pltpu.make_async_copy(stored, weights, scratch[-1])
+    load.start()
+    scratch = scratch[:-1]
     greet([sibling] + partners, after[1:])
     pieces, piece, tokens = left.shape[1:]
     count = own.shape[0]
@@ -203,17 +325,16 @@
             arriving[h].append(copy)
     right[:count] = own[...]
 
-    owned, columns = weights.shape
+    columns, owned = weights.shape
     base = pl.multiple_of(here * owned, 128)
 
     def project(rows, target, first):
         @pl.loop(0, owned // tile)
         def _(i):
             at = pl.multiple_of(i * tile, 128)
-            value = dot(rows[:, :columns], weights[pl.ds(at, tile)], ((1,), (1,)))
+            value = dot(rows[:, :columns], weights[:, pl.ds(at, tile)], ((1,), (0,)))
             target[:, pl.ds(pl.multiple_of(first + at, 128), tile)] = value.astype(BF)
 
-    project(own, grads, base)
 
     def multiply(side, h, target):
         low, high = spans[h]
@@ -273,6 +394,7 @@
             join(k - 1)
             begin(k - 1, 0)
         if k == parts:
+            load.wait()
             for s in range(1, zero):
                 project(right.at[s * count : (s + 1) * count], made.at[s - 1], 0)
                 copy = pltpu.make_async_remote_copy(
@@ -285,6 +407,7 @@
                 )
                 copy.start()
                 returning.append(copy)
+            project(own, grads, base)
         for s in reversed(range(levels)):
             h = k - lag - skew * s
             if 0 <= h < parts:
@@ -303,43 +426,42 @@
     count, cols = own.shape
     zero = tokens // count
     levels = pieces.bit_length() - 1
-    edges = list(range(0, cols, 256)) + [cols]
+    edges = [0] + list(range(128, cols, 256)) + [cols]
     spans = list(zip(edges[:-1], edges[1:]))
     parts = len(spans)
     widths = [high - low for low, high in spans]
-    scratch = [pltpu.VMEM((tokens, cols), BF)]
+    scratch = [pltpu.VMEM((tokens, cols), BF), pltpu.VMEM(weights.shape, BF)]
     scratch += [pltpu.VMEM((pieces, piece, w), F32) for w in widths]
     scratch += [pltpu.VMEM((pieces, piece, w), BF) for w in widths] * 2
     for _ in range(2):
         for w in widths:
             scratch += [pltpu.VMEM((pieces >> (s + 1), piece, w), BF) for s in range(levels)]
-    owned, columns = weights.shape
+    columns, owned = weights.shape
     scratch += [pltpu.VMEM((zero - 1, count, owned), BF)]
     scratch += [pltpu.SemaphoreType.DMA((parts, levels + 1))] * 2
     scratch += [pltpu.SemaphoreType.DMA((parts, zero))] * 2
-    scratch += [pltpu.SemaphoreType.DMA((zero,))] * 2
+    scratch += [pltpu.SemaphoreType.DMA((zero,))] * 2 + [pltpu.SemaphoreType.DMA]
     return pl.pallas_call(
         functools.partial(tail_kernel, spans, min(256, owned)),
         out_shape=(
             jax.ShapeDtypeStruct((piece, columns), F32),
             jax.ShapeDtypeStruct((count, zero * owned), BF),
         ),
-        in_specs=[pl.BlockSpec(memory_space=pltpu.VMEM)] * 3,
+        in_specs=[pl.BlockSpec(memory_space=pltpu.VMEM)] * 2
+        + [pl.BlockSpec(memory_space=pl.ANY)],
         out_specs=[pl.BlockSpec(memory_space=pltpu.VMEM)] * 2,
         scratch_shapes=scratch,
         compiler_params=pltpu.CompilerParams(collective_id=1, has_side_effects=True),
     )(own, left, weights)
 
 
-def ssd_block(proj, gy, a_log, dt_bias, d_skip):
+def ssd_block(xs, joined, raw, gy, guests, a_log, dt_bias, d_skip):
     count, inner = gy.shape
     heads = a_log.shape[0]
     width = inner // heads
-    size = (proj.shape[1] - inner - heads) // 2
-    xs = proj[:, :inner].astype(BF)
-    bm = proj[:, inner : inner + size].astype(BF)
-    cm = proj[:, inner + size : inner + 2 * size].astype(BF)
-    raw = proj[:, inner + 2 * size :] + dt_bias
+    size = joined.shape[1] // 2
+    bm, cm = joined[:, :size], joined[:, size:]
+    raw = raw + dt_bias
     dt = jax.nn.softplus(raw)
     rate = -jnp.exp(a_log)
     lower = jnp.arange(count)[:, None] >= jnp.arange(count)[None, :]
@@ -362,7 +484,9 @@
     marks = jnp.pad(total.reshape(seq, share), ((0, 0), (0, -share % 8)))
     marks = jnp.broadcast_to(marks[:, :, None], marks.shape + (size,))
     marks = marks.reshape(seq // 2, 2, -1, size)
-    start, end = scan_states(pair.reshape(seq // 2, 2, share, 2, width, size), marks)
+    start, end, held = scan_states(
+        pair.reshape(seq // 2, 2, share, 2, width, size), marks, guests
+    )
     start, end = start.reshape(inner, size), end.reshape(inner, size)
 
     spans = cum.T[:, :, None] - cum.T[:, None, :]
@@ -399,35 +523,24 @@
             grad_b,
             grad_c,
             grad_raw,
-            jnp.zeros((count, -proj.shape[1] % 128), F32),
+            jnp.zeros((count, -(inner + 2 * size + heads) % 128), F32),
         ],
         axis=1,
     ).astype(BF)
-    return out.reshape(count, inner).astype(BF), gproj
+    return out.reshape(count, inner).astype(BF), gproj, held
 
 
 def per_device(tokens, w_in, a_log, dt_bias, d_skip, grad_y):
     count, width = tokens.shape[1:]
     inner = grad_y.shape[2]
     heads = a_log.shape[0]
-    columns = w_in.shape[1]
-    exact = columns - heads
     zero = lax.axis_size("zero")
     seq = lax.axis_size("seq")
     here = lax.axis_index("zero")
-    owned = width // zero
     rows = tokens.reshape(count, width)
 
-    def columns_of(z):
-        return lax.dynamic_slice_in_dim(rows, z * owned, owned, axis=1)
-
-    guests = [shift(columns_of((here + s) % zero), "zero", s) for s in range(1, zero)]
-    proj = jnp.dot(columns_of(here), w_in, preferred_element_type=F32)
-    for s, guest in zip(range(1, zero), guests):
-        part = jnp.dot(guest, w_in, preferred_element_type=F32)
-        wide = shift(part[:, :exact].astype(BF), "zero", zero - s)
-        narrow = shift(part[:, exact:], "zero", zero - s)
-        proj = proj + jnp.concatenate([wide.astype(F32), narrow], axis=1)
+    stored = w_in.T
+    xs, joined, raw = head(rows, stored, inner, heads)
 
     piece = width // (seq * zero)
     cut = rows.reshape(count, seq, zero, piece)
@@ -435,13 +548,15 @@
     def pieces_of(z):
         return lax.dynamic_index_in_dim(cut, z, 2, keepdims=False).reshape(count, seq * piece)
 
-    theirs = [shift(pieces_of((here + s) % zero), "zero", s) for s in range(1, zero)]
-
-    y_out, gproj = ssd_block(proj, grad_y.reshape(count, inner), a_log, dt_bias, d_skip)
-
-    left = jnp.concatenate([pieces_of(here)] + theirs, axis=0)
+    guests = jnp.stack([pieces_of((here + s) % zero) for s in range(1, zero)])
+    y_out, gproj, held = ssd_block(
+        xs, joined, raw, grad_y.reshape(count, inner), guests, a_log, dt_bias, d_skip
+    )
+
+    left = jnp.concatenate([pieces_of(here)[None], held], axis=0)
+    left = left.reshape(zero * count, seq * piece)
     left = left.reshape(left.shape[0], seq // 2, 2, piece).transpose(2, 1, 3, 0)
-    grad_w, grad_tokens = tail(gproj, left, w_in)
+    grad_w, grad_tokens = tail(gproj, left, stored)
     grad_tokens = grad_tokens.reshape(1, count, width)
     return (y_out.reshape(1, count, inner), grad_tokens, grad_w)
 

time: 166 us -> 158 us (0.952)
  Pallas kernels: 88.7 us -> 114 us
  waiting for transfers between devices: 14.4 us -> 0 us
  matrix products: 21.1 us -> 11.9 us
  starting transfers between devices: 6.96 us -> 0 us
  local copies, waits for them, and re-layouts: 26.6 us -> 23.4 us
    pallas_call x1 -> x2, Pallas kernels: 33.3 us -> 60.9 us  [the longest x1 33.4 us: scan_states(): pl.pallas_call(scan_kernel, out_shape=(state, state, jax.ShapeDtypeStruct...]
    ppermute x4 -> x0, waiting for transfers between devices: 14.4 us -> none  [shift(): lax.ppermute(value, axis, [(i, (i + step) % count) for i in range(count)])]
    dot_general x2 -> x0, matrix products: 7.84 us -> none  [the longest x1 4.08 us: per_device(): proj = jnp.dot(columns_of(here), w_in, preferred_element_type=F32)]
    unnamed x26 -> x41, local copies, waits for them, and re-layouts: 15.2 us -> 8.27 us
    ppermute x4 -> x0, starting transfers between devices: 6.96 us -> none  [shift(): lax.ppermute(value, axis, [(i, (i + step) % count) for i in range(count)])]
    another operation x0 -> x4, local copies, waits for them, and re-layouts: none -> 6.14 us  [the longest x2 5.14 us: per_device(): left = left.reshape(left.shape[0], seq // 2, 2, piece).transpose(2, 1, 3, 0)]
    pallas_call x1, Pallas kernels: 55.4 us -> 52.8 us  [tail(): pl.pallas_call(functools.partial(tail_kernel, spans, min(256, owned)), ou...]
    transpose x1 -> x0, other arithmetic: 1.82 us -> none  [per_device(): left = left.reshape(left.shape[0], seq // 2, 2, piece).transpose(2, 1, 3, 0)]
  transfers between devices with their start and end apart: 4 -> 0, of which waited for: 2 -> 0; matrix products, arithmetic and copies ran while one was open for 7% -> 0% of each run, Pallas kernels for 0% -> 0%
where the time goes in v3:
time: 158 us; the launch traced here: 157 us
  Pallas kernels  114 us (72%)
  local copies, waits for them, and re-layouts  23.4 us (15%)
  matrix products  11.9 us (8%)
  other arithmetic  6.93 us (4%)
    pallas_call x1, Pallas kernels, tail(): pl.pallas_call(functools.partial(tail_kernel, spans, min(256, owned)), ou...  52.8 us
    pallas_call x1, Pallas kernels, scan_states(): pl.pallas_call(scan_kernel, out_shape=(state, state, jax.ShapeDtypeStruct...  33.4 us
    pallas_call x1, Pallas kernels, head(): pl.pallas_call(functools.partial(head_kernel, zero, inner), out_shape=(ja...  27.5 us
    unnamed x41, local copies, waits for them, and re-layouts  8.27 us
    dot_general x3, matrix products, bdot(): return jnp.einsum(spec, a, b, preferred_element_type=F32)  6.09 us
    dot_general x9, matrix products, dot(): return lax.dot_general(a, b, (dims, ((), ())), preferred_element_type=F32)  5.44 us
    another operation x2, local copies, waits for them, and re-layouts, per_device(): left = left.reshape(left.shape[0], seq // 2, 2, piece).transpose(2, 1, 3, 0)  5.14 us
    mul x2, local copies, waits for them, and re-layouts, ssd_block(): xd = (x3 * dt[:, :, None]).astype(BF)  3.6 us

profile of v3, /device:TPU:0, one launch (start us, length us, event | category | flops | bytes accessed | tf_op | source)
XLA Modules:
  0.0 156.9 jit_solution(11061510895511260576)
XLA Ops:
  0.6 0.7 exponential_negate_fusion
  1.3 1.3 copy.91
  2.7 1.3 copy.92
  4.0 0.1 copy.103
  4.2 0.9 copy.93.guests
  5.0 27.5 %shard_map.85 = (bf16[128,2048]{1,0:T(8,128)(2,1)}, bf16[128,256]{1,0:T(8,128)(2,1)}, f32[128,32]{1,0:T(8,128)}) custom-call(bf16[128,2048]{1,0:T(8,128)(2,1)} %bitcast.104, bf16[2336,1024]{1,0:T(8,128)(2,1)} %bitcast.84), custom_call_target="tpu_custom_call" | custom-call | tf_op jit(solution)/shard_map/pallas_call | solution.py:129
  32.5 0.0 copy-start.2
  32.5 0.0 copy-done.11
  32.5 0.9 compare_select_fusion
  33.5 0.0 copy-done.13
  33.5 0.2 fusion.19
  33.7 0.1 copy.84
  33.8 0.2 slice_reduce_fusion
  34.0 0.1 copy.119
  34.1 0.1 reshape_squeeze.3
  34.2 0.1 subtract_exponential_fusion
  34.2 0.7 broadcast_in_dim.27.totals
  35.0 1.6 fusion.31
  36.5 0.1 fusion.18
  36.6 0.0 copy-done.8
  36.6 1.8 %fusion.4 = bf16[8,2,2,1,64,128]{5,4,3,2,1,0:T(8,128)(2,1)} fusion(bf16[8,2,2,64,128]{4,3,2,1,0:T(8,128)(2,1)S(1)} %bitcast.102, bf16[128,256]{1,0:T(8,128)(2,1)} %get-tuple-element.13), kind=kOutput, calls=%fused_computation.17 | convolution fusion | flops 67371008 | bytes 1081344 | tf_op jit(solution)/shard_map/dot_general | solution.py:21
  38.5 0.0 copy-done.2
  38.5 0.2 copy.82
  38.7 1.0 mul.139
  39.7 1.6 copy.89
  41.3 1.1 mul.131
  42.3 2.5 %copy.87 = f32[128,2048]{1,0:T(8,128)} copy(f32[128,2048]{0,1:T(8,128)} %bitcast.97) | data formatting | bytes 2097152 | tf_op jit(solution)/shard_map/mul | solution.py:474
  44.9 1.6 multiply_convert_fusion.1
  46.4 0.0 copy-start.3
  46.4 0.3 copy.90
  46.7 0.0 copy-done.4
  46.7 0.3 fusion.3
  47.0 0.5 copy-done.3
  47.5 1.1 pad_maximum_fusion.pair
  48.5 33.4 %shard_map.86 = (bf16[8,2,2,64,128]{4,3,2,1,0:T(8,128)(2,1)}, bf16[8,2,2,64,128]{4,3,2,1,0:T(8,128)(2,1)}, bf16[1,128,1024]{2,1,0:T(8,128)(2,1)}) custom-call(bf16[8,2,2,2,64,128]{5,4,3,2,1,0:T(8,128)(2,1)} %pad_maximum_fusion.pair, f32[8,2,8,128]{3,2,1,0:T(8,128)} %broadcast_in_dim.27.totals, bf16[1,128,1024]{2,1,0:T(8,128)(2,1)} %copy.93.guests), custom_call_target="tpu_custom_call" | custom-call | tf_op jit(solution)/shard_map/pallas_call | solution.py:261
  82.0 1.0 pad_maximum_fusion.1
  83.0 0.0 copy-start.1
  83.0 1.5 multiply_reduce_fusion
  84.5 0.1 reduce_sum.65
  84.6 0.0 copy-start.7
  84.6 0.0 copy-start.10
  84.6 1.6 %reshape.143 = bf16[256,8,2,64]{3,2,1,0:T(2,128)(2,1)} reshape(bf16[2,128,1024]{2,1,0:T(8,128)(2,1)S(1)} %pad_maximum_fusion.1) | data formatting | bytes 1048576 | tf_op jit(solution)/shard_map/reshape;reshape | solution.py:558
  86.3 3.5 %copy.105 = bf16[256,8,2,64]{0,3,1,2:T(8,128)(2,1)} copy(bf16[256,8,2,64]{3,2,1,0:T(2,128)(2,1)} %reshape.143) | data formatting | bytes 1048576 | tf_op jit(solution)/shard_map/reshape;reshape | solution.py:558
  89.8 0.0 copy-done.1
  89.8 0.3 fusion.23
  90.1 2.9 %fusion.11 = (f32[128,32]{0,1:T(8,128)}, f32[128,32]{0,1:T(8,128)S(1)}, f32[32]{0:T(128)S(1)}, bf16[128,32,64]{0,2,1:T(8,128)(2,1)S(1)}, bf16[128,32,64]{0,2,1:T(8,128)(2,1)}) fusion(f32[128,2048]{0,1:T(8,128)S(1)} %copy.82, f32[128,32]{0,1:T(8,128)S(1)} %get-tuple-element.43, f32[128,32,64]{0,2,1:T(8,128)S(1)} %fusion.23, f32[128,32,64]{0,2,1:T(8,128)S(1)} %bitcast.94, ...), kind=kOutput, calls=%fused_computation.27 | convolution fusion | flops 74178528 | bytes 4882688 | tf_op jit(solution)/shard_map/hts,thp->shp/dot_general | solution.py:25
  93.0 1.1 fusion
  94.1 0.2 fusion.27
  94.3 0.1 fusion.33
  94.4 0.3 fusion.8
  94.7 0.1 copy.101
  94.8 2.1 %convolution_bitcast_fusion.1 = f32[128,32,64]{0,2,1:T(8,128)S(1)} fusion(bf16[128,32,64]{0,2,1:T(8,128)(2,1)} %copy-done.16, f32[32,128]{1,0:T(8,128)S(1)} %bitcast.111, f32[128,128]{0,1:T(8,128)S(1)} %copy-done.7, pred[128,128]{0,1:T(8,128)(4,1)S(1)} %iota_compare_fusion), kind=kOutput, calls=%fused_computation.11 | convolution fusion | flops 69730304 | bytes 1671168 | tf_op jit(solution)/shard_map/hts,shp->thp/dot_general | solution.py:25
  97.0 0.0 copy-start.12
  97.0 0.0 copy-start.15
  97.0 0.5 fusion.17
  97.5 0.0 copy-start.5
  97.5 0.3 fusion.9
  97.9 0.2 fusion.10
  98.1 1.0 copy.106
  99.1 0.2 copy.102
  99.4 1.0 concatenate.9.own
  100.3 52.8 %shard_map.87 = (f32[64,2336]{1,0:T(8,128)}, bf16[128,2048]{1,0:T(8,128)(2,1)}) custom-call(bf16[128,2432]{1,0:T(8,128)(2,1)} %concatenate.9.own, bf16[2,8,64,256]{3,2,1,0:T(8,128)(2,1)} %bitcast.98, bf16[2336,1024]{1,0:T(8,128)(2,1)} %bitcast.85), custom_call_target="tpu_custom_call" | custom-call | tf_op jit(solution)/shard_map/pallas_call | solution.py:444
  153.1 1.9 %copy.123 = bf16[1,128,2048]{2,1,0:T(8,128)(2,1)} copy(bf16[1,128,2048]{2,1,0:T(8,128)(2,1)} %bitcast.108) | data formatting | bytes 1048576
  155.0 1.9 %copy.124 = f32[64,2336]{1,0:T(8,128)} copy(f32[64,2336]{1,0:T(8,128)} %get-tuple-element.50) | data formatting | bytes 1196032
  (24 shorter events, 0.1 us)
Async XLA Ops:
  1.3 32.2 %copy-start.13 = (f32[32]{0:T(128)}, f32[32]{0:T(128)S(1)}, u32[]{:S(2)}) copy-start(f32[32]{0:T(128)S(1)} %exponential_negate_fusion) | copy-start | bytes 388
  5.0 27.5 %copy-start.11 = (f32[32]{0:T(128)S(1)}, f32[32]{0:T(128)}, u32[]{:S(2)}) copy-start(f32[32]{0:T(128)} %param.9) | copy-start | bytes 388
  32.5 5.9 %copy-start.2 = (bf16[128,2048]{1,0:T(8,128)(2,1)S(1)}, bf16[128,2048]{1,0:T(8,128)(2,1)}, u32[]{:S(2)}) copy-start(bf16[128,2048]{1,0:T(8,128)(2,1)} %get-tuple-element.11) | copy-start | bytes 1572868
  34.0 2.6 %copy-start.8 = (f32[1,32]{1,0:T(1,128)}, f32[1,32]{1,0:T(1,128)S(1)}, u32[]{:S(2)}) copy-start(f32[1,32]{1,0:T(1,128)S(1)} %copy.119) | copy-start | bytes 388
  44.9 1.9 %copy-start.4 = (bf16[128,256]{1,0:T(8,128)(2,1)S(1)}, bf16[128,256]{1,0:T(8,128)(2,1)}, u32[]{:S(2)}) copy-start(bf16[128,256]{1,0:T(8,128)(2,1)} %get-tuple-element.13) | copy-start | bytes 196612
  46.4 1.0 copy-start.3
  83.0 6.8 %copy-start.1 = (bf16[8,2,2,64,128]{4,3,2,1,0:T(8,128)(2,1)S(1)}, bf16[8,2,2,64,128]{4,3,2,1,0:T(8,128)(2,1)}, u32[]{:S(2)}) copy-start(bf16[8,2,2,64,128]{4,3,2,1,0:T(8,128)(2,1)} %get-tuple-element.15) | copy-start | bytes 1572868
  84.6 5.5 %copy-start.7 = (f32[128,128]{0,1:T(8,128)S(1)}, f32[128,128]{0,1:T(8,128)}, u32[]{:S(2)}) copy-start(f32[128,128]{0,1:T(8,128)} %fusion.31) | copy-start | bytes 196612
  84.6 5.5 %copy-start.10 = (f32[32]{0:T(128)S(1)}, f32[32]{0:T(128)}, u32[]{:S(2)}) copy-start(f32[32]{0:T(128)} %param.10) | copy-start | bytes 388
  90.1 2.9 %copy-start.9 = (f32[1,32]{1,0:T(1,128)S(1)}, f32[1,32]{1,0:T(1,128)}, u32[]{:S(2)}) copy-start(f32[1,32]{1,0:T(1,128)} %copy-done.8) | copy-start | bytes 388
  93.0 1.1 copy-start.16
  94.8 2.1 %copy-start = (bf16[8,2,2,64,128]{4,3,2,1,0:T(8,128)(2,1)S(1)}, bf16[8,2,2,64,128]{4,3,2,1,0:T(8,128)(2,1)}, u32[]{:S(2)}) copy-start(bf16[8,2,2,64,128]{4,3,2,1,0:T(8,128)(2,1)} %get-tuple-element.14) | copy-start | bytes 1572868
  97.0 0.9 copy-start.6
  97.0 0.9 copy-start.12
  97.0 0.9 copy-start.14
  97.0 0.9 copy-start.15
  97.5 1.6 %copy-start.5 = (bf16[128,32,64]{0,2,1:T(8,128)(2,1)S(1)}, bf16[128,32,64]{0,2,1:T(8,128)(2,1)}, u32[]{:S(2)}) copy-start(bf16[128,32,64]{0,2,1:T(8,128)(2,1)} %get-tuple-element.35) | copy-start | bytes 1572868

commit v4 on v3

--- a/solution.py
+++ b/solution.py
@@ -10,19 +10,11 @@
 BF = jnp.bfloat16
 F32 = jnp.float32
 MESH = pl.DeviceIdType.MESH
-
-
-def shift(value, axis, step):
-    count = lax.axis_size(axis)
-    return lax.ppermute(value, axis, [(i, (i + step) % count) for i in range(count)])
+LAGS = (0, 1, 3, 5, 6)
 
 
 def dot(a, b, dims):
     return lax.dot_general(a, b, (dims, ((), ())), preferred_element_type=F32)
-
-
-def bdot(a, b, spec):
-    return jnp.einsum(spec, a, b, preferred_element_type=F32)
 
 
 def greet(peers, mates=()):
@@ -151,140 +143,7 @@
     )(rows, weights)
 
 
-def scan_kernel(
-    pair, totals, guests, start, end, held, both, marks, joined, sums, got, lengths, made, back, final, wide,
-    send, recv, local, leave, enter
-):
-    chips, _, share = pair.shape[:3]
-    me = lax.axis_index("seq")
-    core, chip = lax.rem(me, 2), lax.div(me, 2)
-    sibling = me + 1 - 2 * core
-    places = [lax.rem(chip + d, chips) for d in range(1, chips)]
-    peers = [place * 2 + core for place in places]
-    here = lax.axis_index("zero")
-    zero = guests.shape[0] + 1
-    after = [lax.rem(here + s, zero) for s in range(zero)]
-    greet([sibling] + peers, after[1:])
-    crossing = [
-        mate(guests.at[s - 1], held.at[s - 1], leave.at[s - 1], enter.at[s - 1], after[s])
-        for s in range(1, zero)
-    ]
-    for copy in crossing:
-        copy.start()
-
-    def move(copies):
-        for copy in copies:
-            copy.start()
-        for copy in copies:
-            copy.wait()
-
-    move(
-        [
-            remote(pair.at[:, 1 - core], both.at[core], send.at[0, 0], recv.at[0, 0], sibling),
-            remote(totals.at[:, 1 - core], marks.at[core], send.at[1, 0], recv.at[1, 0], sibling),
-            pltpu.make_async_copy(pair.at[:, core], both.at[core], local.at[0]),
-            pltpu.make_async_copy(totals.at[:, core], marks.at[core], local.at[1]),
-        ]
-    )
-
-    def gain(ref, *at):
-        return jnp.exp(ref[at])
-
-    for k in range(chips):
-        sums[k] = marks[0, k] + marks[1, k]
-        for j in range(share):
-            row = pl.ds(j, 1)
-            joined[k, j, 0] = (
-                gain(marks, 1, k, row) * both[0, k, j, 0].astype(F32)
-                + both[1, k, j, 0].astype(F32)
-            ).astype(BF)
-            joined[k, j, 1] = (
-                gain(marks, 0, k, row) * both[1, k, j, 1].astype(F32)
-                + both[0, k, j, 1].astype(F32)
-            ).astype(BF)
-    copies = []
-    for d, (place, peer) in enumerate(zip(places, peers)):
-        copies.append(remote(joined.at[place], got.at[chip], send.at[2, d], recv.at[2, d], peer))
-        copies.append(remote(sums.at[place], lengths.at[chip], send.at[3, d], recv.at[3, d], peer))
-    copies.append(pltpu.make_async_copy(joined.at[chip], got.at[chip], local.at[2]))
-    copies.append(pltpu.make_async_copy(sums.at[chip], lengths.at[chip], local.at[3]))
-    move(copies)
-
-    for j in range(share):
-        row = pl.ds(j, 1)
-        run = jnp.zeros(pair.shape[4:], F32)
-        for k in range(chips):
-            made[k, j, 0] = run.astype(BF)
-            if k < chips - 1:
-                run = gain(lengths, k, row) * run + got[k, j, 0].astype(F32)
-        run = jnp.zeros(pair.shape[4:], F32)
-        for k in reversed(range(chips)):
-            made[k, j, 1] = run.astype(BF)
-            if k > 0:
-                run = gain(lengths, k, row) * run + got[k, j, 1].astype(F32)
-    copies = [
-        remote(made.at[place], back.at[chip], send.at[4, d], recv.at[4, d], peer)
-        for d, (place, peer) in enumerate(zip(places, peers))
-    ]
-    move(copies + [pltpu.make_async_copy(made.at[chip], back.at[chip], local.at[4])])
-
-    for k in range(chips):
-        for j in range(share):
-            row = pl.ds(j, 1)
-            first, last = back[k, j, 0], back[k, j, 1]
-            final[0, k, j, 0] = first
-            final[1, k, j, 1] = last
-            final[1, k, j, 0] = (
-                gain(marks, 0, k, row) * first.astype(F32) + both[0, k, j, 0].astype(F32)
-            ).astype(BF)
-            final[0, k, j, 1] = (
-                gain(marks, 1, k, row) * last.astype(F32) + both[1, k, j, 1].astype(F32)
-            ).astype(BF)
-    move(
-        [
-            remote(final.at[1 - core], wide.at[core], send.at[5, 0], recv.at[5, 0], sibling),
-            pltpu.make_async_copy(final.at[core], wide.at[core], local.at[5]),
-        ]
-    )
-    for parity in range(2):
-        start[:, parity] = wide[parity, :, :, 0]
-        end[:, parity] = wide[parity, :, :, 1]
-    for copy in crossing:
-        copy.wait()
-
-
-def scan_states(pair, totals, guests):
-    chips, _, share, _, rows, lanes = pair.shape
-    state = jax.ShapeDtypeStruct((chips, 2, share, rows, lanes), BF)
-    half = (chips,) + pair.shape[2:]
-    short = (chips,) + totals.shape[2:]
-    return pl.pallas_call(
-        scan_kernel,
-        out_shape=(state, state, jax.ShapeDtypeStruct(guests.shape, BF)),
-        in_specs=[pl.BlockSpec(memory_space=pltpu.VMEM)] * 3,
-        out_specs=[pl.BlockSpec(memory_space=pltpu.VMEM)] * 3,
-        scratch_shapes=[
-            pltpu.VMEM((2,) + half, BF),
-            pltpu.VMEM((2,) + short, F32),
-            pltpu.VMEM(half, BF),
-            pltpu.VMEM(short, F32),
-            pltpu.VMEM(half, BF),
-            pltpu.VMEM(short, F32),
-            pltpu.VMEM(half, BF),
-            pltpu.VMEM(half, BF),
-            pltpu.VMEM((2,) + half, BF),
-            pltpu.VMEM((2,) + half, BF),
-            pltpu.SemaphoreType.DMA((6, chips)),
-            pltpu.SemaphoreType.DMA((6, chips)),
-            pltpu.SemaphoreType.DMA((6,)),
-            pltpu.SemaphoreType.DMA(guests.shape[:1]),
-            pltpu.SemaphoreType.DMA(guests.shape[:1]),
-        ],
-        compiler_params=pltpu.CompilerParams(collective_id=0, has_side_effects=True),
-    )(pair, totals, guests)
-
-
-def tail_kernel(spans, tile, own, left, stored, out, grads, right, weights, *scratch):
+def tail_kernel(spans, tile, own, mine, held, stored, out, grads, right, weights, left, *scratch):
     seq, zero = 2 * left.shape[1], left.shape[3] // own.shape[0]
     levels = (seq // 2).bit_length() - 1
     me, here = lax.axis_index("seq"), lax.axis_index("zero")
@@ -324,6 +183,10 @@
             copy.start()
             arriving[h].append(copy)
     right[:count] = own[...]
+    for way in range(2):
+        for s in range(zero):
+            turned = mine[way].T if s == 0 else held[s - 1, way].T
+            left[way, :, :, s * count : (s + 1) * count] = turned.reshape(pieces, piece, count)
 
     columns, owned = weights.shape
     base = pl.multiple_of(here * owned, 128)
@@ -421,16 +284,17 @@
         copy.wait()
 
 
-def tail(own, left, weights):
-    pieces, piece, tokens = left.shape[1:]
+def tail(own, mine, held, weights, pieces):
     count, cols = own.shape
-    zero = tokens // count
+    zero = held.shape[0] + 1
+    piece, tokens = mine.shape[2] // pieces, zero * count
     levels = pieces.bit_length() - 1
     edges = [0] + list(range(128, cols, 256)) + [cols]
     spans = list(zip(edges[:-1], edges[1:]))
     parts = len(spans)
     widths = [high - low for low, high in spans]
     scratch = [pltpu.VMEM((tokens, cols), BF), pltpu.VMEM(weights.shape, BF)]
+    scratch += [pltpu.VMEM((2, pieces, piece, tokens), BF)]
     scratch += [pltpu.VMEM((pieces, piece, w), F32) for w in widths]
     scratch += [pltpu.VMEM((pieces, piece, w), BF) for w in widths] * 2
     for _ in range(2):
@@ -447,87 +311,338 @@
             jax.ShapeDtypeStruct((piece, columns), F32),
             jax.ShapeDtypeStruct((count, zero * owned), BF),
         ),
-        in_specs=[pl.BlockSpec(memory_space=pltpu.VMEM)] * 2
+        in_specs=[pl.BlockSpec(memory_space=pltpu.VMEM)] * 3
         + [pl.BlockSpec(memory_space=pl.ANY)],
         out_specs=[pl.BlockSpec(memory_space=pltpu.VMEM)] * 2,
         scratch_shapes=scratch,
         compiler_params=pltpu.CompilerParams(collective_id=1, has_side_effects=True),
-    )(own, left, weights)
+    )(own, mine, held, weights)
+
+
+def core_kernel(
+    width, chunk, lags, xs, joined, raws, gy, guests, scalars, y_out, gproj, held,
+    spread, dts, grows, fades, xds, growns, fadeds, ins, backs, cums, turned, mark, marks, gains,
+    loc, both, pairs, duo, sums, far, ret, came, fin, wide,
+    tsend, trecv, send, recv, zsend, zrecv, leave, enter
+):
+    seq, planes = marks.shape[0], far.shape[2]
+    zero = guests.shape[0] + 1
+    me, here = lax.axis_index("seq"), lax.axis_index("zero")
+    core, chip = lax.rem(me, 2), lax.div(me, 2)
+    side, plane = lax.rem(chip, 2), lax.div(chip, 2)
+    sibling, across = me + 1 - 2 * core, me + 2 - 4 * side
+    peers = [lax.rem(me + d, seq) for d in range(1, seq)]
+    after = [lax.rem(here + s, zero) for s in range(zero)]
+    count, inner = xs.shape
+    heads = raws.shape[1]
+    size = joined.shape[1] // 2
+    chunks = inner // chunk
+    high = lax.Precision.HIGHEST
+    far[...] = jnp.zeros(far.shape, BF)
+    mark[...] = jnp.zeros(mark.shape, F32)
+    greet(peers, after[1:])
+    crossing = [
+        mate(guests.at[s - 1], held.at[s - 1], leave.at[s - 1], enter.at[s - 1], after[s])
+        for s in range(1, zero)
+    ]
+    for copy in crossing:
+        copy.start()
+
+    def iota(shape, axis):
+        return lax.broadcasted_iota(jnp.int32, shape, axis)
+
+    lower = iota((count, count), 0) >= iota((count, count), 1)
+    ones = lower.astype(F32)
+    first = iota((heads, inner), 0) * width
+    lane = iota((heads, inner), 1)
+    spread[...] = ((lane >= first) & (lane < first + width)).astype(F32)
+    rate, skip = scalars[0:1, :heads], scalars[2:3, :heads]
+    raw = raws[...] + scalars[1:2, :heads]
+    dt = jnp.maximum(raw, 0.0) + jnp.log1p(jnp.exp(-jnp.abs(raw)))
+    cum = jnp.dot(ones, rate * dt, precision=high, preferred_element_type=F32)
+    total = cum[count - 1 : count]
+    cums[...] = cum
+    turned[...] = cum.T
+    mark[0:1, :heads] = total
+    marks[me] = mark[...]
+    told = [
+        remote(mark, marks.at[me], tsend.at[d], trecv.at[d], peer) for d, peer in enumerate(peers)
+    ]
+    for copy in told:
+        copy.start()
+    growth, fade = jnp.exp(cum), jnp.exp(total - cum)
+    bm, cm = joined[:, :size], joined[:, size:]
+    bt, ct = bm.T, cm.T
+    skips = jnp.broadcast_to(skip, (8, heads))
+
+    def expand(value, low, top):
+        return jnp.dot(value, spread[:, low:top], precision=high, preferred_element_type=F32)
+
+    def gather(value, low, top):
+        return lax.dot_general(
+            value, spread[:, low:top], (((1,), (1,)), ((), ())), precision=high,
+            preferred_element_type=F32,
+        )
+
+    step = min(256, chunk)
+    copies = {}
+
+    def prepare(c):
+        for low in range(c * chunk, (c + 1) * chunk, step):
+            top = low + step
+            own = slice(low - c * chunk, low - c * chunk + step)
+            d, g, f = expand(dt, low, top), expand(growth, low, top), expand(fade, low, top)
+            dts[:, low:top], grows[:, low:top], fades[:, low:top] = d, g, f
+            xd = (xs[:, low:top].astype(F32) * d).astype(BF)
+            grown = (gy[:, low:top].astype(F32) * g).astype(BF)
+            faded = (xd.astype(F32) * f).astype(BF)
+            xds[:, low:top], growns[:, low:top], fadeds[:, low:top] = xd, grown, faded
+            parts = loc.shape[1:2] + loc.shape[3:5] + (step,)
+            loc[c, :, 0, :, :, own] = dot(bt, faded, ((1,), (0,))).astype(BF).reshape(parts)
+            loc[c, :, 1, :, :, own] = dot(ct, grown, ((1,), (0,))).astype(BF).reshape(parts)
+        both[c, core] = loc[c, core]
+        copies[0, c] = remote(
+            loc.at[c, 1 - core], both.at[c, core], send.at[0, c], recv.at[0, c], sibling
+        )
+        copies[0, c].start()
+
+    def gain(c, *rows):
+        at = slice(c * chunk, (c + 1) * chunk)
+        return jnp.exp(sum(gains[pl.ds(row, 1), at] for row in rows))
+
+    def stage_pair(c):
+        copies[0, c].wait()
+        g0, g1 = gain(c, chip * 2), gain(c, chip * 2 + 1)
+        for q in range(2):
+            pairs[c, q, 0] = (
+                g1 * both[c, 0, 0, q].astype(F32) + both[c, 1, 0, q].astype(F32)
+            ).astype(BF)
+            pairs[c, q, 1] = (
+                g0 * both[c, 1, 1, q].astype(F32) + both[c, 0, 1, q].astype(F32)
+            ).astype(BF)
+        duo[c, side] = pairs[c, side]
+        copies[1, c] = remote(
+            pairs.at[c, 1 - side], duo.at[c, side], send.at[1, c], recv.at[1, c], across
+        )
+        copies[1, c].start()
+
+    def along(c, way, d):
+        return remote(
+            sums.at[c, way],
+            far.at[c, way, plane],
+            zsend.at[c, way, d],
+            zrecv.at[c, way, d],
+            me + (4 * d if way == 0 else -4 * d),
+        )
+
+    def later(d, way):
+        return plane + d < planes if way == 0 else plane >= d
+
+    def stage_plane(c):
+        copies[1, c].wait()
+        g0 = gain(c, plane * 4, plane * 4 + 1)
+        g1 = gain(c, plane * 4 + 2, plane * 4 + 3)
+        sums[c, 0] = (g1 * duo[c, 0, 0].astype(F32) + duo[c, 1, 0].astype(F32)).astype(BF)
+        sums[c, 1] = (g0 * duo[c, 1, 1].astype(F32) + duo[c, 0, 1].astype(F32)).astype(BF)
+        for d in range(1, planes):
+            for way in range(2):
+
+                @pl.when(later(d, way))
+                def _():
+                    along(c, way, d).start()
+
+    def stage_far(c):
+        for d in range(1, planes):
+            for way in range(2):
+
+                @pl.when(later(d, 1 - way))
+                def _():
+                    along(c, way, d).wait_recv()
+
+                @pl.when(later(d, way))
+                def _():
+                    along(c, way, d).wait_send()
+
+        at = slice(c * chunk, (c + 1) * chunk)
+        ends = []
+        for way in range(2):
+            run = jnp.zeros(far.shape[3:], F32)
+            for k in range(planes) if way == 0 else reversed(range(planes)):
+                inside = (k < plane if way == 0 else k > plane).astype(F32)
+                whole = sum(gains[4 * k + i : 4 * k + i + 1, at] for i in range(4))
+                run = jnp.exp(whole * inside) * run + far[c, way, k].astype(F32)
+            ends.append(run)
+        g0 = gain(c, plane * 4, plane * 4 + 1)
+        g1 = gain(c, plane * 4 + 2, plane * 4 + 3)
+        ret[c, 0, 0] = ends[0].astype(BF)
+        ret[c, 1, 0] = (g0 * ends[0] + duo[c, 0, 0].astype(F32)).astype(BF)
+        ret[c, 1, 1] = ends[1].astype(BF)
+        ret[c, 0, 1] = (g1 * ends[1] + duo[c, 1, 1].astype(F32)).astype(BF)
+        came[c, side] = ret[c, side]
+        copies[2, c] = remote(
+            ret.at[c, 1 - side], came.at[c, side], send.at[2, c], recv.at[2, c], across
+        )
+        copies[2, c].start()
+
+    def stage_back(c):
+        copies[2, c].wait()
+        g0, g1 = gain(c, chip * 2), gain(c, chip * 2 + 1)
+        for q in range(2):
+            fin[c, 0, 0, q] = came[c, q, 0]
+            fin[c, 1, 1, q] = came[c, q, 1]
+            fin[c, 1, 0, q] = (
+                g0 * came[c, q, 0].astype(F32) + both[c, 0, 0, q].astype(F32)
+            ).astype(BF)
+            fin[c, 0, 1, q] = (
+                g1 * came[c, q, 1].astype(F32) + both[c, 1, 1, q].astype(F32)
+            ).astype(BF)
+        wide[c, core] = fin[c, core]
+        copies[3, c] = remote(
+            fin.at[c, 1 - core], wide.at[c, core], send.at[3, c], recv.at[3, c], sibling
+        )
+        copies[3, c].start()
+
+    scores = dot(cm, bm, ((1,), (1,)))
+    group = 128 // width
+    state = {
+        "mixed": jnp.zeros((count, count), F32),
+        "c": jnp.zeros((count, size), F32),
+        "b": jnp.zeros((count, size), F32),
+        "log": jnp.zeros((count, heads), F32),
+        "dt": jnp.zeros((count, heads), F32),
+        "last": jnp.zeros((8, heads), F32),
+    }
+    place = iota((count, 128), 1)
+    masks = [(place >= width * i) & (place < width * (i + 1)) for i in range(group)]
+
+    def inside(p):
+        low, top = p * 128, (p + 1) * 128
+        x2, g2 = xds[:, low:top], gy[:, low:top]
+        none = jnp.zeros_like(x2)
+        decays = []
+        for i in range(group):
+            h = p * group + i
+            spans = cums[:, h : h + 1] - turned[h : h + 1, :]
+            decays.append(jnp.where(lower, jnp.exp(jnp.where(lower, spans, 0.0)), 0.0))
+        mixing = jnp.concatenate([(scores * decay).astype(BF) for decay in decays], axis=1)
+        stacked = jnp.concatenate([jnp.where(mask, x2, none) for mask in masks], axis=0)
+        ins[:, low:top] = dot(mixing, stacked, ((1,), (0,)))
+        tall = dot(mixing, g2, ((0,), (0,)))
+        back = tall[:count]
+        for i in range(1, group):
+            back = jnp.where(masks[i], tall[i * count : (i + 1) * count], back)
+        backs[:, low:top] = back
+        lifted = jnp.concatenate([jnp.where(mask, g2, none) for mask in masks], axis=0)
+        cross = dot(lifted, x2, ((1,), (1,)))
+        for i in range(group):
+            state["mixed"] += cross[i * count : (i + 1) * count] * decays[i]
+
+    def finish(c):
+        copies[3, c].wait()
+        for low in range(c * chunk, (c + 1) * chunk, step):
+            top = low + step
+            own = slice(low - c * chunk, low - c * chunk + step)
+            start = wide[c, :, 0, :, :, own].reshape(size, step)
+            end = wide[c, :, 1, :, :, own].reshape(size, step)
+            x, g = xs[:, low:top].astype(F32), gy[:, low:top].astype(F32)
+            d, xd = dts[:, low:top], xds[:, low:top].astype(F32)
+            reached = dot(bm, end, ((1,), (0,))) * fades[:, low:top]
+            y3 = ins[:, low:top] + dot(cm, start, ((1,), (0,))) * grows[:, low:top]
+            h3 = backs[:, low:top] + reached
+            kept = expand(skips, low, top)[:1]
+            y_out[:, low:top] = (y3 + kept * x).astype(BF)
+            gproj[:, low:top] = (h3 * d + kept * g).astype(BF)
+            state["c"] += dot(growns[:, low:top], start, ((1,), (1,)))
+            state["b"] += dot(fadeds[:, low:top], end, ((1,), (1,)))
+            state["log"] += gather(g * y3 - xd * h3, low, top)
+            state["dt"] += gather(x * h3, low, top)
+            joint = jnp.sum(start.astype(F32) * end.astype(F32), axis=0, keepdims=True)
+            joint = joint * jnp.exp(gains[pl.ds(me, 1), low:top])
+            last = jnp.sum(xd * reached, axis=0, keepdims=True) + joint
+            state["last"] += gather(jnp.broadcast_to(last, (8, step)), low, top)
+
+    for c in range(chunks):
+        prepare(c)
+    for copy in told:
+        copy.wait()
+    totals = marks[:, 0, :heads]
+    for low in range(0, inner, step):
+        gains[:, low : low + step] = expand(totals, low, low + step)
+    stages = [stage_pair, stage_plane, stage_far, stage_back, finish]
+    steps = chunks + lags[-1]
+    fillers = list(range(inner // 128))
+    per = -(-len(fillers) // lags[-1])
+    for k in range(steps):
+        for lag, stage in reversed(list(zip(lags, stages))):
+            if 0 <= k - lag < chunks:
+                if stage is finish:
+                    while fillers:
+                        inside(fillers.pop(0))
+                stage(k - lag)
+        for _ in range(per):
+            if fillers:
+                inside(fillers.pop(0))
+
+    mixed = state["mixed"].astype(BF)
+    gproj[:, inner : inner + size] = (dot(mixed, cm, ((0,), (0,))) + state["b"]).astype(BF)
+    gproj[:, inner + size : inner + 2 * size] = (
+        dot(mixed, bm, ((1,), (0,))) + state["c"]
+    ).astype(BF)
+    upper = (iota((count, count), 0) <= iota((count, count), 1)).astype(F32)
+    grad_log = jnp.dot(upper, state["log"], precision=high, preferred_element_type=F32)
+    grad_log = grad_log + state["last"][:1]
+    grad_raw = (state["dt"] + grad_log * rate) * jax.nn.sigmoid(raw)
+    edge = inner + 2 * size
+    gproj[:, edge:] = jnp.zeros((count, gproj.shape[1] - edge), BF)
+    gproj[:, edge : edge + heads] = grad_raw.astype(BF)
+    for copy in crossing:
+        copy.wait()
 
 
 def ssd_block(xs, joined, raw, gy, guests, a_log, dt_bias, d_skip):
     count, inner = gy.shape
     heads = a_log.shape[0]
-    width = inner // heads
     size = joined.shape[1] // 2
-    bm, cm = joined[:, :size], joined[:, size:]
-    raw = raw + dt_bias
-    dt = jax.nn.softplus(raw)
-    rate = -jnp.exp(a_log)
-    lower = jnp.arange(count)[:, None] >= jnp.arange(count)[None, :]
-    cum = jnp.dot(lower.astype(F32), rate * dt, precision=lax.Precision.HIGHEST)
-    total = cum[-1]
-    growth = jnp.exp(cum)
-    fade = jnp.exp(total - cum)
-    x3 = xs.reshape(count, heads, width).astype(F32)
-    g3 = gy.reshape(count, heads, width).astype(F32)
-    xd = (x3 * dt[:, :, None]).astype(BF)
-    grown = (g3 * growth[:, :, None]).astype(BF).reshape(count, inner)
-    faded = (xd.astype(F32) * fade[:, :, None]).astype(BF).reshape(count, inner)
-    local_f = dot(faded, bm, ((0,), (0,)))
-    local_g = dot(grown, cm, ((0,), (0,)))
-    shape = (heads, width, size)
-    pair = jnp.stack([local_f.reshape(shape), local_g.reshape(shape)], axis=1).astype(BF)
-
     seq = lax.axis_size("seq")
-    share = heads // seq
-    marks = jnp.pad(total.reshape(seq, share), ((0, 0), (0, -share % 8)))
-    marks = jnp.broadcast_to(marks[:, :, None], marks.shape + (size,))
-    marks = marks.reshape(seq // 2, 2, -1, size)
-    start, end, held = scan_states(
-        pair.reshape(seq // 2, 2, share, 2, width, size), marks, guests
-    )
-    start, end = start.reshape(inner, size), end.reshape(inner, size)
-
-    spans = cum.T[:, :, None] - cum.T[:, None, :]
-    decay = jnp.where(lower[None], jnp.exp(jnp.where(lower[None], spans, 0.0)), 0.0)
-    scores = dot(cm, bm, ((1,), (1,)))
-    mixing = (scores[None] * decay).astype(BF)
-    gb3 = gy.reshape(count, heads, width)
-    y_in = bdot(mixing, xd, "hts,shp->thp")
-    back_in = bdot(mixing, gb3, "hts,thp->shp")
-    cross = bdot(gb3, xd, "thp,shp->hts")
-    mixed = jnp.sum(cross * decay, axis=0).astype(BF)
-
-    y3 = y_in + dot(cm, start, ((1,), (1,))).reshape(x3.shape) * growth[:, :, None]
-    h3 = back_in + dot(bm, end, ((1,), (1,))).reshape(x3.shape) * fade[:, :, None]
-    out = y3 + d_skip[:, None] * x3
-    grad_x = h3 * dt[:, :, None] + d_skip[:, None] * g3
-    grad_c = dot(mixed, bm, ((1,), (0,))) + dot(grown, start, ((1,), (0,)))
-    grad_b = dot(mixed, cm, ((0,), (0,))) + dot(faded, end, ((1,), (0,)))
-    row = jnp.sum(g3 * y3, axis=2)
-    column = jnp.sum(xd.astype(F32) * h3, axis=2)
-    grad_dt = jnp.sum(x3 * h3, axis=2)
-    joint = jnp.sum((start.astype(F32) * end.astype(F32)).reshape(heads, -1), axis=1)
-    tail = jnp.sum(
-        xd.astype(F32) * dot(bm, end, ((1,), (1,))).reshape(x3.shape) * fade[:, :, None], axis=(0, 2)
-    )
-    last = tail + jnp.exp(total) * joint
-    grad_log = jnp.dot(
-        lower.astype(F32).T, row - column, precision=lax.Precision.HIGHEST
-    ) + last
-    grad_raw = (grad_dt + grad_log * rate) * jax.nn.sigmoid(raw)
-    gproj = jnp.concatenate(
-        [
-            grad_x.reshape(count, inner),
-            grad_b,
-            grad_c,
-            grad_raw,
-            jnp.zeros((count, -(inner + 2 * size + heads) % 128), F32),
+    planes = seq // 4
+    chunk = 512
+    chunks = inner // chunk
+    rows = size // 4
+    scalars = jnp.stack([-jnp.exp(a_log), dt_bias, d_skip] + [jnp.zeros_like(a_log)] * 5)
+    padded = -(-(inner + 2 * size + heads) // 128) * 128
+    wide = pltpu.VMEM((count, inner), F32)
+    thin = pltpu.VMEM((count, inner), BF)
+    block = pltpu.VMEM((chunks, 2, 2, 2, rows, chunk), BF)
+    half = pltpu.VMEM((chunks, 2, 2, rows, chunk), BF)
+    dma = pltpu.SemaphoreType.DMA
+    return pl.pallas_call(
+        functools.partial(core_kernel, inner // heads, chunk, LAGS),
+        out_shape=(
+            jax.ShapeDtypeStruct((count, inner), BF),
+            jax.ShapeDtypeStruct((count, padded), BF),
+            jax.ShapeDtypeStruct(guests.shape, BF),
+        ),
+        in_specs=[pl.BlockSpec(memory_space=pltpu.VMEM)] * 6,
+        out_specs=[pl.BlockSpec(memory_space=pltpu.VMEM)] * 3,
+        scratch_shapes=[
+            pltpu.VMEM((heads, inner), F32),
+            wide, wide, wide, thin, thin, thin, wide, wide,
+            pltpu.VMEM((count, heads), F32),
+            pltpu.VMEM((heads, count), F32),
+            pltpu.VMEM((8, 128), F32),
+            pltpu.VMEM((seq, 8, 128), F32),
+            pltpu.VMEM((seq, inner), F32),
+            block, block, half, half,
+            pltpu.VMEM((chunks, 2, rows, chunk), BF),
+            pltpu.VMEM((chunks, 2, planes, rows, chunk), BF),
+            half, half, block, block,
+            dma((seq - 1,)), dma((seq - 1,)),
+            dma((4, chunks)), dma((4, chunks)),
+            dma((chunks, 2, planes)), dma((chunks, 2, planes)),
+            dma(guests.shape[:1]), dma(guests.shape[:1]),
         ],
-        axis=1,
-    ).astype(BF)
-    return out.reshape(count, inner).astype(BF), gproj, held
+        compiler_params=pltpu.CompilerParams(collective_id=0, has_side_effects=True),
+    )(xs, joined, raw, gy, guests, scalars)
 
 
 def per_device(tokens, w_in, a_log, dt_bias, d_skip, grad_y):
@@ -543,20 +658,17 @@
     xs, joined, raw = head(rows, stored, inner, heads)
 
     piece = width // (seq * zero)
-    cut = rows.reshape(count, seq, zero, piece)
+    cut = rows.reshape(count, seq // 2, 2, zero, piece)
 
     def pieces_of(z):
-        return lax.dynamic_index_in_dim(cut, z, 2, keepdims=False).reshape(count, seq * piece)
+        some = lax.dynamic_index_in_dim(cut, z, 3, keepdims=False)
+        return some.transpose(2, 0, 1, 3).reshape(2, count, seq // 2 * piece)
 
     guests = jnp.stack([pieces_of((here + s) % zero) for s in range(1, zero)])
     y_out, gproj, held = ssd_block(
         xs, joined, raw, grad_y.reshape(count, inner), guests, a_log, dt_bias, d_skip
     )
-
-    left = jnp.concatenate([pieces_of(here)[None], held], axis=0)
-    left = left.reshape(zero * count, seq * piece)
-    left = left.reshape(left.shape[0], seq // 2, 2, piece).transpose(2, 1, 3, 0)
-    grad_w, grad_tokens = tail(gproj, left, stored)
+    grad_w, grad_tokens = tail(gproj, pieces_of(here), held, stored, seq // 2)
     grad_tokens = grad_tokens.reshape(1, count, width)
     return (y_out.reshape(1, count, inner), grad_tokens, grad_w)
 

time: 158 us -> 125 us (0.79)
  local copies, waits for them, and re-layouts: 23.4 us -> 8.99 us
  matrix products: 11.9 us -> 0 us
  other arithmetic: 6.93 us -> 0.66 us
    dot_general x14 -> x0, matrix products: 11.9 us -> none  [the longest x3 6.09 us: bdot(): return jnp.einsum(spec, a, b, preferred_element_type=F32)]
    mul x4 -> x0, local copies, waits for them, and re-layouts: 6.19 us -> none  [the longest x2 3.6 us: ssd_block(): xd = (x3 * dt[:, :, None]).astype(BF)]
    pallas_call x1, Pallas kernels: 33.4 us -> 38.4 us  [ssd_block(): pl.pallas_call(functools.partial(core_kernel, inner // heads, chunk, LAGS...]
    pallas_call x1, Pallas kernels: 52.8 us -> 47.9 us  [tail(): pl.pallas_call(functools.partial(tail_kernel, spans, min(256, owned)), ou...]
    another operation x4 -> x3, local copies, waits for them, and re-layouts: 5.37 us -> 1.28 us  [ssd_block(): jnp.stack([-jnp.exp(a_log), dt_bias, d_skip] + [jnp.zeros_like(a_log)] * 5)]
    unnamed x41 -> x6, local copies, waits for them, and re-layouts: 8.27 us -> 5.93 us
    convert_element_type x2 -> x0, other arithmetic: 1.66 us -> none  [the longest x1 1.56 us: ssd_block(): faded = (xd.astype(F32) * fade[:, :, None]).astype(BF).reshape(count, inner)]
where the time goes in v4:
time: 125 us; the launch traced here: 124 us
  Pallas kernels  114 us (91%)
  local copies, waits for them, and re-layouts  8.99 us (7%)
    pallas_call x1, Pallas kernels, tail(): pl.pallas_call(functools.partial(tail_kernel, spans, min(256, owned)), ou...  47.9 us
    pallas_call x1, Pallas kernels, ssd_block(): pl.pallas_call(functools.partial(core_kernel, inner // heads, chunk, LAGS...  38.4 us
    pallas_call x1, Pallas kernels, head(): pl.pallas_call(functools.partial(head_kernel, zero, inner), out_shape=(ja...  27.5 us
    unnamed x6, local copies, waits for them, and re-layouts  5.93 us

profile of v4, /device:TPU:0, one launch (start us, length us, event | category | flops | bytes accessed | tf_op | source)
XLA Modules:
  0.0 124.2 jit_solution(16091521460104780478)
XLA Ops:
  0.6 0.7 negate_bitcast_fusion
  1.3 1.3 %stack.19.scalars = f32[8,32]{1,0:T(8,128)} concatenate(f32[1,32]{1,0:T(1,128)S(1)} %negate_bitcast_fusion, f32[1,32]{1,0:T(1,128)} %bitcast.29, f32[1,32]{1,0:T(1,128)} %bitcast.30, f32[1,32]{1,0:T(1,128)S(1)} %stack_broadcast_in_dim.3, f32[4,32]{1,0:T(4,128)S(1)} %stack.18), dimensions={0} | concatenate | bytes 2048 | tf_op jit(solution)/shard_map/stack | solution.py:611
  2.6 1.3 %copy.14 = bf16[1,128,2048]{1,2,0:T(8,128)(2,1)S(1)} copy(bf16[1,128,2048]{2,1,0:T(8,128)(2,1)} %param.6) | data formatting | bytes 1048576 | tf_op args[0]
  4.0 0.9 copy.18.mine
  4.9 0.9 copy.16.guests
  5.7 27.5 %shard_map.85 = (bf16[128,2048]{1,0:T(8,128)(2,1)}, bf16[128,256]{1,0:T(8,128)(2,1)}, f32[128,32]{1,0:T(8,128)}) custom-call(bf16[128,2048]{1,0:T(8,128)(2,1)} %bitcast.23, bf16[2336,1024]{1,0:T(8,128)(2,1)} %bitcast.20), custom_call_target="tpu_custom_call" | custom-call | tf_op jit(solution)/shard_map/pallas_call | solution.py:121
  33.2 38.4 %shard_map.86 = (bf16[128,2048]{1,0:T(8,128)(2,1)}, bf16[128,2432]{1,0:T(8,128)(2,1)}, bf16[1,2,128,512]{3,2,1,0:T(8,128)(2,1)}) custom-call(bf16[128,2048]{1,0:T(8,128)(2,1)} %get-tuple-element.11.xs, bf16[128,256]{1,0:T(8,128)(2,1)} %get-tuple-element.12.joined, f32[128,32]{1,0:T(8,128)} %get-tuple-element.13.raws, bf16[128,2048]{1,0:T(8,128)(2,1)} %bitcast.28, ...), custom_call_target="tpu_custom_call" | custom-call | tf_op jit(solution)/shard_map/pallas_call | solution.py:618
  71.7 0.0 copy-start
  71.7 47.9 %shard_map.87 = (f32[64,2336]{1,0:T(8,128)}, bf16[128,2048]{1,0:T(8,128)(2,1)}) custom-call(bf16[128,2432]{1,0:T(8,128)(2,1)} %get-tuple-element.15.own, bf16[2,128,512]{2,1,0:T(8,128)(2,1)} %copy.18.mine, bf16[1,2,128,512]{3,2,1,0:T(8,128)(2,1)} %get-tuple-element.16.held, bf16[2336,1024]{1,0:T(8,128)(2,1)} %bitcast.21), custom_call_target="tpu_custom_call" | custom-call | tf_op jit(solution)/shard_map/pallas_call | solution.py:308
  119.6 0.0 copy-done
  119.6 0.8 copy.22
  120.4 1.9 %copy.23 = bf16[1,128,2048]{2,1,0:T(8,128)(2,1)} copy(bf16[1,128,2048]{2,1,0:T(8,128)(2,1)} %bitcast.27) | data formatting | bytes 1048576
  122.3 1.9 %copy.24 = f32[64,2336]{1,0:T(8,128)} copy(f32[64,2336]{1,0:T(8,128)} %get-tuple-element.26) | data formatting | bytes 1196032
  (5 shorter events, 0.1 us)
Async XLA Ops:
  71.7 48.0 %copy-start = (bf16[128,2048]{1,0:T(8,128)(2,1)S(1)}, bf16[128,2048]{1,0:T(8,128)(2,1)}, u32[]{:S(2)}) copy-start(bf16[128,2048]{1,0:T(8,128)(2,1)} %get-tuple-element.14) | copy-start | bytes 1572868
